TPU v7x, 32 devices: a whole 2x2x4 slice. The times are simulated.
32 devices in a mesh: expert: 16 (over z, y, x), store: 2 (over core).
Axes of the slice: x: 2, y: 2, z: 4, core: 2. Of those that a mesh axis runs over, the one named last changes fastest.
Arguments:
- tokens: bfloat16 [4096, 2048], P(('expert', 'store')), may hold values from -6 to 6
- chosen_expert_index: int32 [4096, 8], P(('expert', 'store')), may hold values from 0 to 15, all different within a row; in each aligned block of 128 rows (0 to 127, 128 to 255, ...) at most 72 rows name the same one
- router_weight_logits: float32 [4096, 8], P(('expert', 'store')), may hold values from 0.1 to 1
- token_tenant_index: int32 [4096], P(('expert', 'store')), may hold values from 0 to 1
- adapted: int32 [2, 16], P(None, 'expert'), may hold values 0 or 1
- gate_up_weight: bfloat16 [16, 2048, 768], P('expert', 'store'), may hold values from -0.125 to 0.125
- down_weight: bfloat16 [16, 384, 2048], P('expert', None, 'store'), may hold values from -0.3125 to 0.3125
- adapter_input_factors: bfloat16 [2, 16, 32, 2048], P('store', 'expert'), may hold values from -0.125 to 0.125
- adapter_output_factors: bfloat16 [2, 16, 32, 384], P('store', 'expert'), may hold values from -0.8984375 to 0.8984375
Outputs:
- mixed: bfloat16 [4096, 2048], P(('expert', 'store'))
Inputs may be any that keep to these rules, and one draw needn't show every extreme that they name: `chosen_expert_index`: each row names 8 different experts; within the rows of one device no expert is named by more than 72 rows.
All inputs are finite; a program needn't handle non-finite values. No bound on the sum of `adapted` on one device may be relied on, other than what follows from the above.
Results may differ from a plain program's by a relative error of at most 0.006.
Values may be sent and summed in bfloat16 or wider, within the bound.
No kernel may reach another device: no remote copies, remote signals or barrier semaphores. Data moves between devices by JAX's collectives and lax.ppermute only.
A program may use at most 128 MiB of HBM per device.

v0:
```python
import functools

import jax
import jax.numpy as jnp
from jax import lax
from jax.experimental import pallas as pl
from jax.experimental.pallas import tpu as pltpu
from jax.sharding import Mesh, PartitionSpec as P


F32 = jnp.float32
BF16 = jnp.bfloat16
LANES = 128
INNER = 4
VMEM = pl.BlockSpec(memory_space=pltpu.VMEM)
SMEM = pl.BlockSpec(memory_space=pltpu.SMEM)


def call(body, outs, ins, flops, cost_bytes):
    smem = ins[0]
    return pl.pallas_call(
        body,
        out_shape=outs,
        in_specs=[SMEM] * len(smem) + [VMEM] * (len(ins) - 1),
        out_specs=jax.tree.map(lambda _: VMEM, outs),
        compiler_params=pltpu.CompilerParams(vmem_limit_bytes=20 * 1024 * 1024),
        cost_estimate=pl.CostEstimate(flops=flops, bytes_accessed=cost_bytes, transcendentals=0),
    )(*smem, *ins[1:])


def iota(shape, dim):
    return lax.broadcasted_iota(jnp.int32, shape, dim)


def packing(meta, expert, top):
    tok = meta.shape[0]
    lane = iota(meta.shape, 1)
    chosen = jnp.where(lane < top, meta, -1.0)
    named = jnp.zeros(meta.shape, F32)
    hits = []
    for q in range(INNER):
        target = lax.bitwise_xor(expert, q).astype(F32)
        hit = jnp.max(jnp.where(chosen == target, 1.0, 0.0), axis=1, keepdims=True)
        hits.append(hit)
        named = jnp.where(lane == q, hit, named)
    below = jnp.where(iota((tok, tok), 1) < iota((tok, tok), 0), 1.0, 0.0).astype(BF16)
    place = jnp.dot(below, named.astype(BF16), preferred_element_type=F32)
    slots = []
    for q in range(INNER):
        slot = jnp.where(hits[q] > 0.0, place[:, q : q + 1], -1.0)
        slots.append(slot)
    return slots


def one_hot(slots, rows):
    tok = slots[0].shape[0]
    lane = iota((tok, INNER * rows), 1).astype(F32)
    picked = jnp.zeros((tok, INNER * rows), F32)
    for q in range(INNER):
        at = jnp.where(slots[q] >= 0.0, slots[q] + float(q * rows), -1.0)
        picked = jnp.where(lane == at, 1.0, picked)
    return picked.astype(BF16)


def pack_rows(slots, wide, outs, rows):
    picked = one_hot(slots, rows)
    got = lax.dot_general(picked, wide, (((0,), (0,)), ((), ())), preferred_element_type=F32).astype(BF16)
    for q in range(INNER):
        outs[q][...] = got[q * rows : (q + 1) * rows]


def first_body(top, rows, expert_ref, tok_any, meta_ref, ext_ref, *refs):
    outs, sem = refs[:INNER], refs[INNER]
    tok, width = tok_any.shape
    copy = pltpu.make_async_copy(tok_any, ext_ref.at[:, pl.ds(0, width)], sem)
    copy.start()
    logits = meta_ref[top + 8 :]
    share = logits / jnp.sum(logits, axis=0, keepdims=True)
    high = share.astype(BF16).astype(F32)
    mid = (share - high).astype(BF16).astype(F32)
    low = share - high - mid
    pad = jnp.zeros((32 - top, tok), F32)
    meta_t = jnp.concatenate(
        [
            meta_ref[: top + 8],
            jnp.zeros((32 - top - 8, tok), F32),
            high,
            pad,
            mid,
            pad,
            low,
            pad,
        ],
        axis=0,
    )
    meta = meta_t.T
    ext_ref[:, width:] = meta.astype(BF16)
    slots = packing(meta, expert_ref[0], top)
    copy.wait()
    pack_rows(slots, ext_ref[...], outs, rows)


def either(scal_ref, pair, columns=slice(None)):
    return jnp.where(scal_ref[2] > 0, pair[1][:, columns], pair[0][:, columns])


def pack_body(top, rows, width, scal_ref, inner_ref, end_ref, *outs):
    wide = either(scal_ref, (inner_ref, end_ref))
    pack_rows(packing(wide[:, width:].astype(F32), scal_ref[0], top), wide, outs, rows)


def expert_body(top, rows, stores, parts, scal_ref, adapted_ref, *refs):
    xs, refs = refs[:INNER], refs[INNER:]
    ups, refs = refs[:stores], refs[stores:]
    downs, refs = refs[:stores], refs[stores:]
    fins, refs = refs[:stores], refs[stores:]
    fups, refs = refs[:stores], refs[stores:]
    outs, (x_ref, fin_ref, fup_ref, y_ref) = refs[: INNER * parts], refs[INNER * parts :]
    store = scal_ref[1]
    width = ups[0].shape[0] * stores
    hidden = downs[0].shape[0]
    for q in range(INNER):
        x_ref[q * rows : (q + 1) * rows] = xs[q][...]
    k = ups[0].shape[0]
    pre = None
    for r in range(stores):
        at = pl.multiple_of(lax.bitwise_xor(store, r) * k, LANES)
        part = jnp.dot(x_ref[:, pl.ds(at, k)], ups[r][...], preferred_element_type=F32)
        pre = part if pre is None else pre + part
    tenants = adapted_ref.shape[0]
    held = tenants // stores
    part = fins[0].shape[0]
    rank = part // held
    for r in range(stores):
        fin_ref[r * part : (r + 1) * part] = fins[r][...]
        fup_ref[r * part : (r + 1) * part] = fups[r][...]
    lane = iota((1, stores * part), 1)
    half = (lane % rank) < rank // 2
    tenant = lax.bitwise_xor(store, lane // part) * held + (lane // rank) % held
    allowed = jnp.zeros(lane.shape, F32)
    for u in range(tenants):
        allowed = jnp.where(tenant == u, adapted_ref[u].astype(F32), allowed)
    code = x_ref[:, width + top : width + top + 1].astype(F32)
    low = lax.dot_general(
        x_ref[:, :width], fin_ref[...], (((1,), (1,)), ((), ())), preferred_element_type=F32
    )
    low = (low * jnp.where(code == tenant.astype(F32), allowed, 0.0)).astype(BF16)
    zero = jnp.zeros_like(low)
    gate = pre[:, :hidden] + jnp.dot(jnp.where(half, low, zero), fup_ref[...], preferred_element_type=F32)
    up = pre[:, hidden:] + jnp.dot(jnp.where(half, zero, low), fup_ref[...], preferred_element_type=F32)
    act = (gate / (1.0 + jnp.exp(-gate)) * up).astype(BF16)
    n = downs[0].shape[1]
    for r in range(stores):
        at = pl.multiple_of(lax.bitwise_xor(store, r) * n, LANES)
        y_ref[:, pl.ds(at, n)] = jnp.dot(act, downs[r][...], preferred_element_type=F32).astype(BF16)
    each = width // parts
    for q in range(INNER):
        for i in range(parts):
            outs[q * parts + i][...] = y_ref[q * rows : (q + 1) * rows, i * each : (i + 1) * each]


def weighted(expert, meta, ys, top, rows):
    slots = packing(meta, expert, top)
    lane = iota(meta.shape, 1)
    chosen = jnp.where(lane < top, meta, -1.0)
    share = sum(pltpu.roll(meta, LANES - 32 * (i + 1), 1) for i in range(3))
    total = None
    for q in range(INNER):
        target = lax.bitwise_xor(expert, q).astype(F32)
        mine = jnp.sum(jnp.where(chosen == target, share, 0.0), axis=1, keepdims=True)
        spot = iota((meta.shape[0], rows), 1).astype(F32)
        spread = jnp.where(spot == slots[q], 1.0, 0.0).astype(BF16)
        part = jnp.dot(spread, ys[q][...], preferred_element_type=F32) * mine
        total = part if total is None else total + part
    return total


def partial_body(top, rows, width, scal_ref, inner_ref, end_ref, *refs):
    meta = either(scal_ref, (inner_ref, end_ref), slice(width, None)).astype(F32)
    refs[INNER][...] = weighted(scal_ref[0], meta, refs[:INNER], top, rows).astype(BF16)


def final_body(top, rows, width, splits, expert_ref, ext_ref, *refs):
    meta = ext_ref[:, width:].astype(F32)
    total = weighted(expert_ref[0], meta, refs[:INNER], top, rows)
    others, out = list(refs[INNER:-1]), refs[-1]
    for count in splits:
        pieces = [others.pop(0)[...].astype(F32) for _ in range(count)]
        total = total + (pieces[0] if count == 1 else jnp.concatenate(pieces, axis=1))
    out[...] = total.astype(BF16)


def swap(array, axis, distance):
    return lax.ppermute(array, axis, [(i, i ^ distance) for i in range(lax.axis_size(axis))])


def spread(block, outer):
    if outer != 4:
        return [(block, block)] + [(got, got) for got in (swap(block, "outer", d) for d in range(1, outer))]
    middle, outward = [(1, 2), (2, 1)], [(1, 0), (2, 3)]
    near = swap(block, "outer", 1)
    over = lax.ppermute(block, "outer", middle)
    over_near = lax.ppermute(near, "outer", middle)
    end_over = lax.ppermute(over, "outer", outward)
    end_over_near = lax.ppermute(over_near, "outer", outward)
    return [(block, block), (near, near), (over, end_over), (over_near, end_over_near)]


def column_parts(d, outer):
    return 2 if outer == 4 and d in (2, 3) else 1


def shards(
    tokens,
    chosen_expert_index,
    router_weight_logits,
    token_tenant_index,
    adapted,
    gate_up_weight,
    down_weight,
    adapter_input_factors,
    adapter_output_factors,
):
    tok, width = tokens.shape
    top = chosen_expert_index.shape[1]
    outer, stores = lax.axis_size("outer"), lax.axis_size("store")
    owners = outer * INNER
    cap = max(2, tok * top * 9 // (8 * owners))
    rows = -(-cap // 8) * 8
    hidden = down_weight.shape[1]
    wide = width + LANES
    expert = lax.axis_index("outer") * INNER + lax.axis_index("inner")
    store = lax.axis_index("store")
    place = lax.axis_index("outer")
    ends = jnp.logical_or(place == 0, place == outer - 1)
    scal = jnp.stack([expert, store, ends.astype(jnp.int32)]).astype(jnp.int32)
    packed = jax.ShapeDtypeStruct((rows, wide), BF16)
    ext_shape = jax.ShapeDtypeStruct((tok, wide), BF16)
    sums = jax.ShapeDtypeStruct((tok, width), BF16)

    move_flops = 2 * tok * INNER * rows * width
    move_bytes = 2 * (tok + INNER * rows) * wide
    meta = jnp.concatenate(
        [
            chosen_expert_index.T.astype(F32),
            jnp.broadcast_to(token_tenant_index.astype(F32), (8, tok)),
            router_weight_logits.T,
        ]
    )
    first = pl.pallas_call(
        functools.partial(first_body, top, rows),
        out_shape=[ext_shape] + [packed] * INNER,
        in_specs=[SMEM, pl.BlockSpec(memory_space=pl.ANY), VMEM],
        out_specs=[VMEM] * (1 + INNER),
        scratch_shapes=[pltpu.SemaphoreType.DMA],
        compiler_params=pltpu.CompilerParams(vmem_limit_bytes=20 * 1024 * 1024),
        cost_estimate=pl.CostEstimate(flops=move_flops, bytes_accessed=move_bytes, transcendentals=0),
        name="first",
    )(scal, tokens, meta)
    blocks = spread(first[0], outer)
    rows_of = [first[1:]]

    ups = [gate_up_weight[0]]
    downs = [down_weight[0]]
    fin = [adapter_input_factors.reshape(-1, width)]
    fup = [adapter_output_factors.reshape(-1, hidden)]
    for r in range(1, stores):
        ups.append(swap(ups[0], "store", r))
        downs.append(swap(downs[0], "store", r))
        fin.append(swap(fin[0], "store", r))
        fup.append(swap(fup[0], "store", r))

    for d in range(1, outer):
        rows_of.append(
            call(
                functools.partial(pack_body, top, rows, width),
                [packed] * INNER,
                [[scal], *blocks[d]],
                move_flops,
                move_bytes,
            )
        )
    arrived = [[r[0]] + [swap(r[q], "inner", q) for q in range(1, INNER)] for r in rows_of]

    backs = []
    for d in range(outer):
        parts = column_parts(d, outer)
        kernel = pl.pallas_call(
            functools.partial(expert_body, top, rows, stores, parts),
            out_shape=[jax.ShapeDtypeStruct((rows, width // parts), BF16)] * (INNER * parts),
            in_specs=[SMEM] * 2 + [VMEM] * (INNER + 4 * stores),
            out_specs=[VMEM] * (INNER * parts),
            scratch_shapes=[
                pltpu.VMEM((INNER * rows, wide), BF16),
                pltpu.VMEM((stores * fin[0].shape[0], width), BF16),
                pltpu.VMEM((stores * fin[0].shape[0], hidden), BF16),
                pltpu.VMEM((INNER * rows, width), BF16),
            ],
            compiler_params=pltpu.CompilerParams(vmem_limit_bytes=28 * 1024 * 1024),
            cost_estimate=pl.CostEstimate(
                flops=2 * INNER * rows * width * hidden * 3, bytes_accessed=6 * width * hidden, transcendentals=0
            ),
            name="expert",
        )
        got = kernel(scal, adapted[:, 0], *arrived[d], *ups, *downs, *fin, *fup)
        backs.append([[got[i]] + [swap(got[q * parts + i], "inner", q) for q in range(1, INNER)] for i in range(parts)])

    def partial(d, i=0):
        return call(
            functools.partial(partial_body, top, rows, width),
            jax.ShapeDtypeStruct((tok, width // len(backs[d])), BF16),
            [[scal], *blocks[d], *backs[d][i]],
            move_flops,
            move_bytes,
        )

    if outer == 4:
        others = []
        for d, targets in ((2, [(1, 2), (2, 1)]), (3, [(1, 3), (2, 0)])):
            others.append([])
            for i in range(len(backs[d])):
                part = partial(d, i)
                more = lax.ppermute(part, "outer", [(0, 1), (3, 2)])
                part = (part.astype(F32) + more.astype(F32)).astype(BF16)
                others[-1].append(lax.ppermute(part, "outer", targets))
        others.append([swap(partial(1), "outer", 1)])
    else:
        others = [[swap(partial(d), "outer", d)] for d in range(1, outer)]
    return call(
        functools.partial(final_body, top, rows, width, [len(other) for other in others]),
        sums,
        [[scal], first[0]] + backs[0][0] + sum(others, []),
        move_flops,
        move_bytes,
    )


def solution(mesh):
    owners, stores = mesh.devices.shape
    grid = Mesh(mesh.devices.reshape(owners // INNER, INNER, stores), ("outer", "inner", "store"))
    expert, both = ("outer", "inner"), ("outer", "inner", "store")
    placed = (
        P(both, None),
        P(both, None),
        P(both, None),
        P(both),
        P(None, expert),
        P(expert, "store", None),
        P(expert, None, "store"),
        P("store", expert, None, None),
        P("store", expert, None, None),
    )

    return jax.shard_map(shards, mesh=grid, in_specs=placed, out_specs=P(both, None), check_vma=False)
```

profile of v0, /device:TPU:0, one launch (start us, length us, event | category | flops | bytes accessed | tf_op | source)
XLA Modules:
  0.0 174.3 jit_solution(14751875448175442198)
XLA Ops:
  3.3 1.6 first.1
  6.3 5.4 %collective-permute-start.25 = (bf16[128,2176]{1,0:T(8,128)(2,1)S(1)}, bf16[128,2176]{1,0:T(8,128)(2,1)S(1)}, u32[]{:S(2)}, u32[]{:S(2)}) collective-permute-start(bf16[128,2176]{1,0:T(8,128)(2,1)S(1)} %get-tuple-element.46.ext_ref), channel_id=1, source_target_pairs={{0,8},{8,0},{16,24},{24,16},{1,9},{9,1},{17,25},{25,17},{2,10},{10... | collective-permute-start | bytes 1671176 | tf_op jit(solution)/shard_map/ppermute | solution.py:194
  13.2 11.7 %collective-permute-done.25.inner_ref.end_ref = bf16[128,2176]{1,0:T(8,128)(2,1)S(1)} collective-permute-done((bf16[128,2176]{1,0:T(8,128)(2,1)S(1)}, bf16[128,2176]{1,0:T(8,128)(2,1)S(1)}, u32[]{:S(2)}, u32[]{:S(2)}) %collective-permute-start.25) | collective-permute-done | bytes 557088 | tf_op jit(solution)/shard_map/ppermute | solution.py:194
  30.1 7.2 %collective-permute-done.11.end_ref = bf16[128,2176]{1,0:T(8,128)(2,1)S(1)} collective-permute-done((bf16[128,2176]{1,0:T(8,128)(2,1)S(1)}, bf16[128,2176]{1,0:T(8,128)(2,1)S(1)}, u32[]{:S(2)}, u32[]{:S(2)}) %collective-permute-start.11) | collective-permute-done | bytes 557088 | tf_op jit(solution)/shard_map/ppermute | solution.py:204
  41.9 3.1 %collective-permute-done.1.refs_2_ = bf16[72,2176]{1,0:T(8,128)(2,1)S(1)} collective-permute-done((bf16[72,2176]{1,0:T(8,128)(2,1)S(1)}, bf16[72,2176]{1,0:T(8,128)(2,1)S(1)}, u32[]{:S(2)}, u32[]{:S(2)}) %collective-permute-start.1) | collective-permute-done | bytes 313376 | tf_op jit(solution)/shard_map/ppermute | solution.py:194
  50.9 1.6 collective-permute-start.2
  52.4 13.0 %collective-permute-done.13.refs_2_ = bf16[72,2176]{1,0:T(8,128)(2,1)S(1)} collective-permute-done((bf16[72,2176]{1,0:T(8,128)(2,1)S(1)}, bf16[72,2176]{1,0:T(8,128)(2,1)S(1)}, u32[]{:S(2)}, u32[]{:S(2)}) %collective-permute-start.13) | collective-permute-done | bytes 313376 | tf_op jit(solution)/shard_map/ppermute | solution.py:194
  68.9 3.0 %expert.5 = (bf16[72,1024]{1,0:T(8,128)(2,1)S(1)}, bf16[72,1024]{1,0:T(8,128)(2,1)S(1)}, bf16[72,1024]{1,0:T(8,128)(2,1)S(1)}, bf16[72,1024]{1,0:T(8,128)(2,1)S(...) custom-call(s32[3]{0:T(128)S(1)} %pad_add_fusion.expert_ref.scal_ref, ...), custom_call_target="tpu_custom_call" | custom-call | flops 1358954496 | bytes 4718592 | tf_op jit(solution)/shard_map/expert/pallas_call | solution.py:305
  71.9 1.6 collective-permute-start.15
  73.5 2.1 %collective-permute-done.41.refs_1_ = bf16[72,2176]{1,0:T(8,128)(2,1)S(1)} collective-permute-done((bf16[72,2176]{1,0:T(8,128)(2,1)S(1)}, bf16[72,2176]{1,0:T(8,128)(2,1)S(1)}, u32[]{:S(2)}, u32[]{:S(2)}) %collective-permute-start.41) | collective-permute-done | bytes 313376 | tf_op jit(solution)/shard_map/ppermute | solution.py:194
  80.2 3.7 %collective-permute-done.42.refs_2_ = bf16[72,2176]{1,0:T(8,128)(2,1)S(1)} collective-permute-done((bf16[72,2176]{1,0:T(8,128)(2,1)S(1)}, bf16[72,2176]{1,0:T(8,128)(2,1)S(1)}, u32[]{:S(2)}, u32[]{:S(2)}) %collective-permute-start.42) | collective-permute-done | bytes 313376 | tf_op jit(solution)/shard_map/ppermute | solution.py:194
  84.1 1.9 %collective-permute-start.29 = (bf16[72,2176]{1,0:T(8,128)(2,1)S(1)}, bf16[72,2176]{1,0:T(8,128)(2,1)S(1)}, u32[]{:S(2)}, u32[]{:S(2)}) collective-permute-start(bf16[72,2176]{1,0:T(8,128)(2,1)S(1)} %get-tuple-element.69), channel_id=1, source_target_pairs={{0,4},{2,6},{4,0},{6,2},{1,5},{3,7},{5,1},{7,3},{8,12},{10,14},{12... | collective-permute-start | bytes 940040 | tf_op jit(solution)/shard_map/ppermute | solution.py:194
  87.6 1.6 collective-permute-start.21
  89.6 1.6 collective-permute-start.30
  91.2 3.0 %expert.7 = (bf16[72,2048]{1,0:T(8,128)(2,1)S(1)}, bf16[72,2048]{1,0:T(8,128)(2,1)S(1)}, bf16[72,2048]{1,0:T(8,128)(2,1)S(1)}, bf16[72,2048]{1,0:T(8,128)(2,1)S(1)}) custom-call(s32[3]{0:T(128)S(1)} %pad_add_fusion.expert_ref.scal_ref, s32[2]{0:T(128)S(1)} %bitcast.32, bf16[72,2176]{1,0:T(8,128)(2,1)S(1)} %get-tuple-element.79.refs_0_, ...), custom_call_target="tpu_custom_call" | custom-call | flops 1358954496 | bytes 4718592 | tf_op jit(solution)/shard_map/expert/pallas_call | solution.py:305
  94.2 4.5 %collective-permute-done.20.refs_1_ = bf16[72,1024]{1,0:T(8,128)(2,1)S(1)} collective-permute-done((bf16[72,1024]{1,0:T(8,128)(2,1)S(1)}, bf16[72,1024]{1,0:T(8,128)(2,1)S(1)}, u32[]{:S(2)}, u32[]{:S(2)}) %collective-permute-start.20) | collective-permute-done | bytes 147488 | tf_op jit(solution)/shard_map/ppermute | solution.py:194
  100.2 2.2 %collective-permute-start.45 = (bf16[72,2048]{1,0:T(8,128)(2,1)S(1)}, bf16[72,2048]{1,0:T(8,128)(2,1)S(1)}, u32[]{:S(2)}, u32[]{:S(2)}) collective-permute-start(bf16[72,2048]{1,0:T(8,128)(2,1)S(1)} %get-tuple-element.85), channel_id=1, source_target_pairs={{0,4},{2,6},{4,0},{6,2},{1,5},{3,7},{5,1},{7,3},{8,12},{10,14},{12... | collective-permute-start | bytes 884744 | tf_op jit(solution)/shard_map/ppermute | solution.py:194
  103.0 2.3 %collective-permute-start.22 = (bf16[72,1024]{1,0:T(8,128)(2,1)S(1)}, bf16[72,1024]{1,0:T(8,128)(2,1)S(1)}, u32[]{:S(2)}, u32[]{:S(2)}) collective-permute-start(bf16[72,1024]{1,0:T(8,128)(2,1)S(1)} %get-tuple-element.66), channel_id=1, source_target_pairs={{0,6},{2,4},{4,2},{6,0},{1,7},{3,5},{5,3},{7,1},{8,14},{10,12},{12... | collective-permute-start | bytes 442376 | tf_op jit(solution)/shard_map/ppermute | solution.py:194
  106.6 3.8 %collective-permute-start.18 = (bf16[128,1024]{1,0:T(8,128)(2,1)S(1)}, bf16[128,1024]{1,0:T(8,128)(2,1)S(1)}, u32[]{:S(2)}, u32[]{:S(2)}) collective-permute-start(bf16[128,1024]{1,0:T(8,128)(2,1)S(1)} %shard_map.92), channel_id=1, source_target_pairs={{0,8},{24,16},{1,9},{25,17},{2,10},{26,18},{3,11},{27,19},{4,12},{... | collective-permute-start | bytes 786440 | tf_op jit(solution)/shard_map/ppermute | solution.py:323
  110.5 3.0 %expert.6 = (bf16[72,1024]{1,0:T(8,128)(2,1)S(1)}, bf16[72,1024]{1,0:T(8,128)(2,1)S(1)}, bf16[72,1024]{1,0:T(8,128)(2,1)S(1)}, bf16[72,1024]{1,0:T(8,128)(2,1)S(...) custom-call(s32[3]{0:T(128)S(1)} %pad_add_fusion.expert_ref.scal_ref, ...), custom_call_target="tpu_custom_call" | custom-call | flops 1358954496 | bytes 4718592 | tf_op jit(solution)/shard_map/expert/pallas_call | solution.py:305
  113.5 6.5 %collective-permute-done.22.refs_3_ = bf16[72,1024]{1,0:T(8,128)(2,1)S(1)} collective-permute-done((bf16[72,1024]{1,0:T(8,128)(2,1)S(1)}, bf16[72,1024]{1,0:T(8,128)(2,1)S(1)}, u32[]{:S(2)}, u32[]{:S(2)}) %collective-permute-start.22) | collective-permute-done | bytes 147488 | tf_op jit(solution)/shard_map/ppermute | solution.py:194
  121.5 2.0 %collective-permute-start.33 = (bf16[72,1024]{1,0:T(8,128)(2,1)S(1)}, bf16[72,1024]{1,0:T(8,128)(2,1)S(1)}, u32[]{:S(2)}, u32[]{:S(2)}) collective-permute-start(bf16[72,1024]{1,0:T(8,128)(2,1)S(1)} %get-tuple-element.74), channel_id=1, source_target_pairs={{0,6},{2,4},{4,2},{6,0},{1,7},{3,5},{5,3},{7,1},{8,14},{10,12},{12... | collective-permute-start | bytes 442376 | tf_op jit(solution)/shard_map/ppermute | solution.py:194
  123.5 3.0 %expert.4 = (bf16[72,2048]{1,0:T(8,128)(2,1)S(1)}, bf16[72,2048]{1,0:T(8,128)(2,1)S(1)}, bf16[72,2048]{1,0:T(8,128)(2,1)S(1)}, bf16[72,2048]{1,0:T(8,128)(2,1)S(1)}) custom-call(s32[3]{0:T(128)S(1)} %pad_add_fusion.expert_ref.scal_ref, s32[2]{0:T(128)S(1)} %bitcast.34, bf16[72,2176]{1,0:T(8,128)(2,1)S(1)} %get-tuple-element.47.refs_0_, ...), custom_call_target="tpu_custom_call" | custom-call | flops 1358954496 | bytes 4718592 | tf_op jit(solution)/shard_map/expert/pallas_call | solution.py:305
  129.2 1.6 shard_map.98
  132.4 1.9 %collective-permute-start.38 = (bf16[72,1024]{1,0:T(8,128)(2,1)S(1)}, bf16[72,1024]{1,0:T(8,128)(2,1)S(1)}, u32[]{:S(2)}, u32[]{:S(2)}) collective-permute-start(bf16[72,1024]{1,0:T(8,128)(2,1)S(1)} %get-tuple-element.78), channel_id=1, source_target_pairs={{0,6},{2,4},{4,2},{6,0},{1,7},{3,5},{5,3},{7,1},{8,14},{10,12},{12... | collective-permute-start | bytes 442376 | tf_op jit(solution)/shard_map/ppermute | solution.py:194
  139.1 2.3 %collective-permute-done.37.refs_2_ = bf16[72,1024]{1,0:T(8,128)(2,1)S(1)} collective-permute-done((bf16[72,1024]{1,0:T(8,128)(2,1)S(1)}, bf16[72,1024]{1,0:T(8,128)(2,1)S(1)}, u32[]{:S(2)}, u32[]{:S(2)}) %collective-permute-start.37) | collective-permute-done | bytes 147488 | tf_op jit(solution)/shard_map/ppermute | solution.py:194
  141.3 1.8 %collective-permute-start.9 = (bf16[72,2048]{1,0:T(8,128)(2,1)S(1)}, bf16[72,2048]{1,0:T(8,128)(2,1)S(1)}, u32[]{:S(2)}, u32[]{:S(2)}) collective-permute-start(bf16[72,2048]{1,0:T(8,128)(2,1)S(1)} %get-tuple-element.54), channel_id=1, source_target_pairs={{0,6},{2,4},{4,2},{6,0},{1,7},{3,5},{5,3},{7,1},{8,14},{10,12},{12... | collective-permute-start | bytes 884744 | tf_op jit(solution)/shard_map/ppermute | solution.py:194
  146.2 5.1 %collective-permute-done.39 = bf16[128,1024]{1,0:T(8,128)(2,1)S(1)} collective-permute-done((bf16[128,1024]{1,0:T(8,128)(2,1)S(1)}, bf16[128,1024]{1,0:T(8,128)(2,1)S(1)}, u32[]{:S(2)}, u32[]{:S(2)}) %collective-permute-start.39) | collective-permute-done | bytes 262176 | tf_op jit(solution)/shard_map/ppermute | solution.py:323
  155.4 3.6 %collective-permute-done.47.refs_8_ = bf16[128,2048]{1,0:T(8,128)(2,1)S(1)} collective-permute-done((bf16[128,2048]{1,0:T(8,128)(2,1)S(1)}, bf16[128,2048]{1,0:T(8,128)(2,1)S(1)}, u32[]{:S(2)}, u32[]{:S(2)}) %collective-permute-start.47) | collective-permute-done | bytes 524320 | tf_op jit(solution)/shard_map/ppermute | solution.py:194
  159.1 9.9 %collective-permute-done.35.refs_6_ = bf16[128,1024]{1,0:T(8,128)(2,1)S(1)} collective-permute-done((bf16[128,1024]{1,0:T(8,128)(2,1)S(1)}, bf16[128,1024]{1,0:T(8,128)(2,1)S(1)}, u32[]{:S(2)}, u32[]{:S(2)}) %collective-permute-start.35) | collective-permute-done | bytes 262176 | tf_op jit(solution)/shard_map/ppermute | solution.py:325
  169.0 2.8 %collective-permute-done.40.refs_7_ = bf16[128,1024]{1,0:T(8,128)(2,1)S(1)} collective-permute-done((bf16[128,1024]{1,0:T(8,128)(2,1)S(1)}, bf16[128,1024]{1,0:T(8,128)(2,1)S(1)}, u32[]{:S(2)}, u32[]{:S(2)}) %collective-permute-start.40) | collective-permute-done | bytes 262176 | tf_op jit(solution)/shard_map/ppermute | solution.py:325
  171.8 2.6 %shard_map.99 = bf16[128,2048]{1,0:T(8,128)(2,1)} custom-call(s32[3]{0:T(128)S(1)} %pad_add_fusion.expert_ref.scal_ref, bf16[128,2176]{1,0:T(8,128)(2,1)S(1)} %get-tuple-element.46.ext_ref, bf16[72,2048]{1,0:T(8,128)(2,1)S(1)} %get-tuple-element.51.refs_0_, bf16[72,2048]{1,0:T(8,128)(2,1)S(1)} %collective-permute-done.7.refs_1_, ...), custom_call_target="tpu_custom_call" | custom-call | flops 150994944 | bytes 1810432 | tf_op jit(solution)/shard_map/pallas_call | solution.py:21
  (99 shorter events, 52.8 us)
Async XLA Ops:
  5.7 62.7 %collective-permute-start.3 = (bf16[1024,768]{1,0:T(8,128)(2,1)}, bf16[1024,768]{1,0:T(8,128)(2,1)S(1)}, u32[]{:S(2)}, u32[]{:S(2)}) collective-permute-start(bf16[1024,768]{1,0:T(8,128)(2,1)} %bitcast.11), channel_id=1, source_target_pairs={{0,1},{1,0},{2,3},{3,2},{4,5},{5,4},{6,7},{7,6},{8,9},{9,8},{10,11... | collective-permute-start | bytes 4718600 | tf_op jit(solution)/shard_map/ppermute | solution.py:194
  6.3 18.7 %collective-permute-start.25 = (bf16[128,2176]{1,0:T(8,128)(2,1)S(1)}, bf16[128,2176]{1,0:T(8,128)(2,1)S(1)}, u32[]{:S(2)}, u32[]{:S(2)}) collective-permute-start(bf16[128,2176]{1,0:T(8,128)(2,1)S(1)} %get-tuple-element.46.ext_ref), channel_id=1, source_target_pairs={{0,8},{8,0},{16,24},{24,16},{1,9},{9,1},{17,25},{25,17},{2,10},{10... | collective-permute-start | bytes 1671176 | tf_op jit(solution)/shard_map/ppermute | solution.py:194
  11.7 25.6 %collective-permute-start.11 = (bf16[128,2176]{1,0:T(8,128)(2,1)S(1)}, bf16[128,2176]{1,0:T(8,128)(2,1)S(1)}, u32[]{:S(2)}, u32[]{:S(2)}) collective-permute-start(bf16[128,2176]{1,0:T(8,128)(2,1)S(1)} %collective-permute-done.10.inner_ref), channel_id=1, source_target_pairs={{8,0},{16,24},{9,1},{17,25},{10,2},{18,26},{11,3},{19,27},{12,4},{... | collective-permute-start | bytes 1671176 | tf_op jit(solution)/shard_map/ppermute | solution.py:204
  13.0 34.9 %collective-permute-start.4 = (bf16[384,1024]{1,0:T(8,128)(2,1)}, bf16[384,1024]{1,0:T(8,128)(2,1)S(1)}, u32[]{:S(2)}, u32[]{:S(2)}) collective-permute-start(bf16[384,1024]{1,0:T(8,128)(2,1)} %bitcast.16), channel_id=1, source_target_pairs={{0,1},{1,0},{2,3},{3,2},{4,5},{5,4},{6,7},{7,6},{8,9},{9,8},{10,11... | collective-permute-start | bytes 2359304 | tf_op jit(solution)/shard_map/ppermute | solution.py:194
  24.9 21.7 %collective-permute-start.26 = (bf16[128,2176]{1,0:T(8,128)(2,1)S(1)}, bf16[128,2176]{1,0:T(8,128)(2,1)S(1)}, u32[]{:S(2)}, u32[]{:S(2)}) collective-permute-start(bf16[128,2176]{1,0:T(8,128)(2,1)S(1)} %collective-permute-done.25.inner_ref.end_ref), channel_id=1, source_target_pairs={{8,16},{16,8},{9,17},{17,9},{10,18},{18,10},{11,19},{19,11},{12,20... | collective-permute-start | bytes 1671176 | tf_op jit(solution)/shard_map/ppermute | solution.py:203
  28.6 11.7 %collective-permute-start = (bf16[72,2176]{1,0:T(8,128)(2,1)S(1)}, bf16[72,2176]{1,0:T(8,128)(2,1)S(1)}, u32[]{:S(2)}, u32[]{:S(2)}) collective-permute-start(bf16[72,2176]{1,0:T(8,128)(2,1)S(1)} %get-tuple-element.48), channel_id=1, source_target_pairs={{0,2},{2,0},{4,6},{6,4},{1,3},{3,1},{5,7},{7,5},{8,10},{10,8},{12,... | collective-permute-start | bytes 940040 | tf_op jit(solution)/shard_map/ppermute | solution.py:194
  45.0 20.4 %collective-permute-start.13 = (bf16[72,2176]{1,0:T(8,128)(2,1)S(1)}, bf16[72,2176]{1,0:T(8,128)(2,1)S(1)}, u32[]{:S(2)}, u32[]{:S(2)}) collective-permute-start(bf16[72,2176]{1,0:T(8,128)(2,1)S(1)} %get-tuple-element.57), channel_id=1, source_target_pairs={{0,4},{2,6},{4,0},{6,2},{1,5},{3,7},{5,1},{7,3},{8,12},{10,14},{12... | collective-permute-start | bytes 940040 | tf_op jit(solution)/shard_map/ppermute | solution.py:194
  46.6 30.6 %collective-permute-start.27 = (bf16[128,2176]{1,0:T(8,128)(2,1)S(1)}, bf16[128,2176]{1,0:T(8,128)(2,1)S(1)}, u32[]{:S(2)}, u32[]{:S(2)}) collective-permute-start(bf16[128,2176]{1,0:T(8,128)(2,1)S(1)} %collective-permute-done.26.inner_ref), channel_id=1, source_target_pairs={{8,0},{16,24},{9,1},{17,25},{10,2},{18,26},{11,3},{19,27},{12,4},{... | collective-permute-start | bytes 1671176 | tf_op jit(solution)/shard_map/ppermute | solution.py:205
  47.9 19.0 %collective-permute-start.14 = (bf16[72,2176]{1,0:T(8,128)(2,1)S(1)}, bf16[72,2176]{1,0:T(8,128)(2,1)S(1)}, u32[]{:S(2)}, u32[]{:S(2)}) collective-permute-start(bf16[72,2176]{1,0:T(8,128)(2,1)S(1)} %get-tuple-element.58), channel_id=1, source_target_pairs={{0,6},{2,4},{4,2},{6,0},{1,7},{3,5},{5,3},{7,1},{8,14},{10,12},{12... | collective-permute-start | bytes 940040 | tf_op jit(solution)/shard_map/ppermute | solution.py:194
  50.9 21.0 %collective-permute-start.2 = (bf16[72,2176]{1,0:T(8,128)(2,1)S(1)}, bf16[72,2176]{1,0:T(8,128)(2,1)S(1)}, u32[]{:S(2)}, u32[]{:S(2)}) collective-permute-start(bf16[72,2176]{1,0:T(8,128)(2,1)S(1)} %get-tuple-element.50), channel_id=1, source_target_pairs={{0,6},{2,4},{4,2},{6,0},{1,7},{3,5},{5,3},{7,1},{8,14},{10,12},{12... | collective-permute-start | bytes 940040 | tf_op jit(solution)/shard_map/ppermute | solution.py:194
  66.9 17.0 %collective-permute-start.42 = (bf16[72,2176]{1,0:T(8,128)(2,1)S(1)}, bf16[72,2176]{1,0:T(8,128)(2,1)S(1)}, u32[]{:S(2)}, u32[]{:S(2)}) collective-permute-start(bf16[72,2176]{1,0:T(8,128)(2,1)S(1)} %get-tuple-element.81), channel_id=1, source_target_pairs={{0,4},{2,6},{4,0},{6,2},{1,5},{3,7},{5,1},{7,3},{8,12},{10,14},{12... | collective-permute-start | bytes 940040 | tf_op jit(solution)/shard_map/ppermute | solution.py:194
  68.4 15.7 %collective-permute-start.43 = (bf16[72,2176]{1,0:T(8,128)(2,1)S(1)}, bf16[72,2176]{1,0:T(8,128)(2,1)S(1)}, u32[]{:S(2)}, u32[]{:S(2)}) collective-permute-start(bf16[72,2176]{1,0:T(8,128)(2,1)S(1)} %get-tuple-element.82), channel_id=1, source_target_pairs={{0,6},{2,4},{4,2},{6,0},{1,7},{3,5},{5,3},{7,1},{8,14},{10,12},{12... | collective-permute-start | bytes 940040 | tf_op jit(solution)/shard_map/ppermute | solution.py:194
  71.9 14.1 %collective-permute-start.15 = (bf16[72,1024]{1,0:T(8,128)(2,1)S(1)}, bf16[72,1024]{1,0:T(8,128)(2,1)S(1)}, u32[]{:S(2)}, u32[]{:S(2)}) collective-permute-start(bf16[72,1024]{1,0:T(8,128)(2,1)S(1)} %get-tuple-element.60), channel_id=1, source_target_pairs={{0,2},{2,0},{4,6},{6,4},{1,3},{3,1},{5,7},{7,5},{8,10},{10,8},{12,... | collective-permute-start | bytes 442376 | tf_op jit(solution)/shard_map/ppermute | solution.py:194
  75.7 12.0 %collective-permute-start.16 = (bf16[72,1024]{1,0:T(8,128)(2,1)S(1)}, bf16[72,1024]{1,0:T(8,128)(2,1)S(1)}, u32[]{:S(2)}, u32[]{:S(2)}) collective-permute-start(bf16[72,1024]{1,0:T(8,128)(2,1)S(1)} %get-tuple-element.61), channel_id=1, source_target_pairs={{0,4},{2,6},{4,0},{6,2},{1,5},{3,7},{5,1},{7,3},{8,12},{10,14},{12... | collective-permute-start | bytes 442376 | tf_op jit(solution)/shard_map/ppermute | solution.py:194
  77.1 12.5 %collective-permute-start.17 = (bf16[72,1024]{1,0:T(8,128)(2,1)S(1)}, bf16[72,1024]{1,0:T(8,128)(2,1)S(1)}, u32[]{:S(2)}, u32[]{:S(2)}) collective-permute-start(bf16[72,1024]{1,0:T(8,128)(2,1)S(1)} %get-tuple-element.62), channel_id=1, source_target_pairs={{0,6},{2,4},{4,2},{6,0},{1,7},{3,5},{5,3},{7,1},{8,14},{10,12},{12... | collective-permute-start | bytes 442376 | tf_op jit(solution)/shard_map/ppermute | solution.py:194
  83.9 18.5 %collective-permute-start.28 = (bf16[72,2176]{1,0:T(8,128)(2,1)S(1)}, bf16[72,2176]{1,0:T(8,128)(2,1)S(1)}, u32[]{:S(2)}, u32[]{:S(2)}) collective-permute-start(bf16[72,2176]{1,0:T(8,128)(2,1)S(1)} %get-tuple-element.68), channel_id=1, source_target_pairs={{0,2},{2,0},{4,6},{6,4},{1,3},{3,1},{5,7},{7,5},{8,10},{10,8},{12,... | collective-permute-start | bytes 940040 | tf_op jit(solution)/shard_map/ppermute | solution.py:194
  84.1 18.9 %collective-permute-start.29 = (bf16[72,2176]{1,0:T(8,128)(2,1)S(1)}, bf16[72,2176]{1,0:T(8,128)(2,1)S(1)}, u32[]{:S(2)}, u32[]{:S(2)}) collective-permute-start(bf16[72,2176]{1,0:T(8,128)(2,1)S(1)} %get-tuple-element.69), channel_id=1, source_target_pairs={{0,4},{2,6},{4,0},{6,2},{1,5},{3,7},{5,1},{7,3},{8,12},{10,14},{12... | collective-permute-start | bytes 940040 | tf_op jit(solution)/shard_map/ppermute | solution.py:194
  86.0 12.6 %collective-permute-start.20 = (bf16[72,1024]{1,0:T(8,128)(2,1)S(1)}, bf16[72,1024]{1,0:T(8,128)(2,1)S(1)}, u32[]{:S(2)}, u32[]{:S(2)}) collective-permute-start(bf16[72,1024]{1,0:T(8,128)(2,1)S(1)} %get-tuple-element.64), channel_id=1, source_target_pairs={{0,2},{2,0},{4,6},{6,4},{1,3},{3,1},{5,7},{7,5},{8,10},{10,8},{12,... | collective-permute-start | bytes 442376 | tf_op jit(solution)/shard_map/ppermute | solution.py:194
  87.6 12.5 %collective-permute-start.21 = (bf16[72,1024]{1,0:T(8,128)(2,1)S(1)}, bf16[72,1024]{1,0:T(8,128)(2,1)S(1)}, u32[]{:S(2)}, u32[]{:S(2)}) collective-permute-start(bf16[72,1024]{1,0:T(8,128)(2,1)S(1)} %get-tuple-element.65), channel_id=1, source_target_pairs={{0,4},{2,6},{4,0},{6,2},{1,5},{3,7},{5,1},{7,3},{8,12},{10,14},{12... | collective-permute-start | bytes 442376 | tf_op jit(solution)/shard_map/ppermute | solution.py:194
  89.6 17.0 %collective-permute-start.30 = (bf16[72,2176]{1,0:T(8,128)(2,1)S(1)}, bf16[72,2176]{1,0:T(8,128)(2,1)S(1)}, u32[]{:S(2)}, u32[]{:S(2)}) collective-permute-start(bf16[72,2176]{1,0:T(8,128)(2,1)S(1)} %get-tuple-element.70), channel_id=1, source_target_pairs={{0,6},{2,4},{4,2},{6,0},{1,7},{3,5},{5,3},{7,1},{8,14},{10,12},{12... | collective-permute-start | bytes 940040 | tf_op jit(solution)/shard_map/ppermute | solution.py:194
  98.6 22.9 %collective-permute-start.44 = (bf16[72,2048]{1,0:T(8,128)(2,1)S(1)}, bf16[72,2048]{1,0:T(8,128)(2,1)S(1)}, u32[]{:S(2)}, u32[]{:S(2)}) collective-permute-start(bf16[72,2048]{1,0:T(8,128)(2,1)S(1)} %get-tuple-element.84), channel_id=1, source_target_pairs={{0,2},{2,0},{4,6},{6,4},{1,3},{3,1},{5,7},{7,5},{8,10},{10,8},{12,... | collective-permute-start | bytes 884744 | tf_op jit(solution)/shard_map/ppermute | solution.py:194
  100.2 21.4 %collective-permute-start.45 = (bf16[72,2048]{1,0:T(8,128)(2,1)S(1)}, bf16[72,2048]{1,0:T(8,128)(2,1)S(1)}, u32[]{:S(2)}, u32[]{:S(2)}) collective-permute-start(bf16[72,2048]{1,0:T(8,128)(2,1)S(1)} %get-tuple-element.85), channel_id=1, source_target_pairs={{0,4},{2,6},{4,0},{6,2},{1,5},{3,7},{5,1},{7,3},{8,12},{10,14},{12... | collective-permute-start | bytes 884744 | tf_op jit(solution)/shard_map/ppermute | solution.py:194
  102.4 25.5 %collective-permute-start.46 = (bf16[72,2048]{1,0:T(8,128)(2,1)S(1)}, bf16[72,2048]{1,0:T(8,128)(2,1)S(1)}, u32[]{:S(2)}, u32[]{:S(2)}) collective-permute-start(bf16[72,2048]{1,0:T(8,128)(2,1)S(1)} %get-tuple-element.86), channel_id=1, source_target_pairs={{0,6},{2,4},{4,2},{6,0},{1,7},{3,5},{5,3},{7,1},{8,14},{10,12},{12... | collective-permute-start | bytes 884744 | tf_op jit(solution)/shard_map/ppermute | solution.py:194
  103.0 17.0 %collective-permute-start.22 = (bf16[72,1024]{1,0:T(8,128)(2,1)S(1)}, bf16[72,1024]{1,0:T(8,128)(2,1)S(1)}, u32[]{:S(2)}, u32[]{:S(2)}) collective-permute-start(bf16[72,1024]{1,0:T(8,128)(2,1)S(1)} %get-tuple-element.66), channel_id=1, source_target_pairs={{0,6},{2,4},{4,2},{6,0},{1,7},{3,5},{5,3},{7,1},{8,14},{10,12},{12... | collective-permute-start | bytes 442376 | tf_op jit(solution)/shard_map/ppermute | solution.py:194
  106.6 29.0 %collective-permute-start.18 = (bf16[128,1024]{1,0:T(8,128)(2,1)S(1)}, bf16[128,1024]{1,0:T(8,128)(2,1)S(1)}, u32[]{:S(2)}, u32[]{:S(2)}) collective-permute-start(bf16[128,1024]{1,0:T(8,128)(2,1)S(1)} %shard_map.92), channel_id=1, source_target_pairs={{0,8},{24,16},{1,9},{25,17},{2,10},{26,18},{3,11},{27,19},{4,12},{... | collective-permute-start | bytes 786440 | tf_op jit(solution)/shard_map/ppermute | solution.py:323
  127.8 16.6 %collective-permute-start.23 = (bf16[128,1024]{1,0:T(8,128)(2,1)S(1)}, bf16[128,1024]{1,0:T(8,128)(2,1)S(1)}, u32[]{:S(2)}, u32[]{:S(2)}) collective-permute-start(bf16[128,1024]{1,0:T(8,128)(2,1)S(1)} %shard_map.93), channel_id=1, source_target_pairs={{0,8},{24,16},{1,9},{25,17},{2,10},{26,18},{3,11},{27,19},{4,12},{... | collective-permute-start | bytes 786440 | tf_op jit(solution)/shard_map/ppermute | solution.py:323
  137.6 14.5 %collective-permute-start.7 = (bf16[72,2048]{1,0:T(8,128)(2,1)S(1)}, bf16[72,2048]{1,0:T(8,128)(2,1)S(1)}, u32[]{:S(2)}, u32[]{:S(2)}) collective-permute-start(bf16[72,2048]{1,0:T(8,128)(2,1)S(1)} %get-tuple-element.52), channel_id=1, source_target_pairs={{0,2},{2,0},{4,6},{6,4},{1,3},{3,1},{5,7},{7,5},{8,10},{10,8},{12,... | collective-permute-start | bytes 884744 | tf_op jit(solution)/shard_map/ppermute | solution.py:194
  141.3 11.5 %collective-permute-start.8 = (bf16[72,2048]{1,0:T(8,128)(2,1)S(1)}, bf16[72,2048]{1,0:T(8,128)(2,1)S(1)}, u32[]{:S(2)}, u32[]{:S(2)}) collective-permute-start(bf16[72,2048]{1,0:T(8,128)(2,1)S(1)} %get-tuple-element.53), channel_id=1, source_target_pairs={{0,4},{2,6},{4,0},{6,2},{1,5},{3,7},{5,1},{7,3},{8,12},{10,14},{12... | collective-permute-start | bytes 884744 | tf_op jit(solution)/shard_map/ppermute | solution.py:194
  141.3 12.8 %collective-permute-start.9 = (bf16[72,2048]{1,0:T(8,128)(2,1)S(1)}, bf16[72,2048]{1,0:T(8,128)(2,1)S(1)}, u32[]{:S(2)}, u32[]{:S(2)}) collective-permute-start(bf16[72,2048]{1,0:T(8,128)(2,1)S(1)} %get-tuple-element.54), channel_id=1, source_target_pairs={{0,6},{2,4},{4,2},{6,0},{1,7},{3,5},{5,3},{7,1},{8,14},{10,12},{12... | collective-permute-start | bytes 884744 | tf_op jit(solution)/shard_map/ppermute | solution.py:194
  145.8 13.2 %collective-permute-start.47 = (bf16[128,2048]{1,0:T(8,128)(2,1)S(1)}, bf16[128,2048]{1,0:T(8,128)(2,1)S(1)}, u32[]{:S(2)}, u32[]{:S(2)}) collective-permute-start(bf16[128,2048]{1,0:T(8,128)(2,1)S(1)} %shard_map.98), channel_id=1, source_target_pairs={{0,8},{8,0},{16,24},{24,16},{1,9},{9,1},{17,25},{25,17},{2,10},{10... | collective-permute-start | bytes 1572872 | tf_op jit(solution)/shard_map/ppermute | solution.py:194
  152.8 16.2 %collective-permute-start.35 = (bf16[128,1024]{1,0:T(8,128)(2,1)S(1)}, bf16[128,1024]{1,0:T(8,128)(2,1)S(1)}, u32[]{:S(2)}, u32[]{:S(2)}) collective-permute-start(bf16[128,1024]{1,0:T(8,128)(2,1)S(1)} %add_convert_fusion.1), channel_id=1, source_target_pairs={{8,24},{16,0},{9,25},{17,1},{10,26},{18,2},{11,27},{19,3},{12,28},... | collective-permute-start | bytes 786440 | tf_op jit(solution)/shard_map/ppermute | solution.py:325
  154.1 17.7 %collective-permute-start.40 = (bf16[128,1024]{1,0:T(8,128)(2,1)S(1)}, bf16[128,1024]{1,0:T(8,128)(2,1)S(1)}, u32[]{:S(2)}, u32[]{:S(2)}) collective-permute-start(bf16[128,1024]{1,0:T(8,128)(2,1)S(1)} %add_convert_fusion), channel_id=1, source_target_pairs={{8,24},{16,0},{9,25},{17,1},{10,26},{18,2},{11,27},{19,3},{12,28},... | collective-permute-start | bytes 786440 | tf_op jit(solution)/shard_map/ppermute | solution.py:325
  (22 other events, 465.3 us)
where the time goes:
time: 175 us; the launch traced here: 174 us
  waiting for transfers between devices  79.8 us (46%)
  starting transfers between devices  63 us (36%)
  Pallas kernels  27.5 us (16%)
  other arithmetic  2.53 us (1%)
    ppermute x36, waiting for transfers between devices, swap(): lax.ppermute(array, axis, [(i, i ^ distance) for i in range(lax.axis_size...  54.7 us
    ppermute x36, starting transfers between devices, swap(): lax.ppermute(array, axis, [(i, i ^ distance) for i in range(lax.axis_size...  47.4 us
    pallas_call x9, Pallas kernels, call(): pl.pallas_call(body, out_shape=outs, in_specs=[SMEM] * len(smem) + [VMEM]...  13.9 us
    ppermute x4, waiting for transfers between devices, shards(): others[-1].append(lax.ppermute(part, 'outer', targets))  12.7 us
    pallas_call x4, Pallas kernels, shards(): got = kernel(scal, adapted[:, 0], *arrived[d], *ups, *downs, *fin, *fup)  12 us
    ppermute x4, starting transfers between devices, shards(): more = lax.ppermute(part, 'outer', [(0, 1), (3, 2)])  7.76 us
    ppermute x1, waiting for transfers between devices, spread(): end_over = lax.ppermute(over, 'outer', outward)  7.21 us
    ppermute x4, waiting for transfers between devices, shards(): more = lax.ppermute(part, 'outer', [(0, 1), (3, 2)])  5.15 us
  transfers between devices with their start and end apart: 48, of which 18 were waited for; matrix products, arithmetic and copies ran while one was open for 0% of the time, Pallas kernels for 13%

commit v1 on v0

--- a/solution.py
+++ b/solution.py
@@ -100,13 +100,9 @@
     pack_rows(slots, ext_ref[...], outs, rows)
 
 
-def either(scal_ref, pair, columns=slice(None)):
-    return jnp.where(scal_ref[2] > 0, pair[1][:, columns], pair[0][:, columns])
-
-
-def pack_body(top, rows, width, scal_ref, inner_ref, end_ref, *outs):
-    wide = either(scal_ref, (inner_ref, end_ref))
-    pack_rows(packing(wide[:, width:].astype(F32), scal_ref[0], top), wide, outs, rows)
+def pack_body(top, rows, width, scal_ref, *refs):
+    wide = either(scal_ref, refs[:-INNER])
+    pack_rows(packing(wide[:, width:].astype(F32), scal_ref[0], top), wide, refs[-INNER:], rows)
 
 
 def expert_body(top, rows, stores, parts, scal_ref, adapted_ref, *refs):
@@ -175,14 +171,17 @@
     return total
 
 
-def partial_body(top, rows, width, scal_ref, inner_ref, end_ref, *refs):
-    meta = either(scal_ref, (inner_ref, end_ref), slice(width, None)).astype(F32)
-    refs[INNER][...] = weighted(scal_ref[0], meta, refs[:INNER], top, rows).astype(BF16)
-
-
-def final_body(top, rows, width, splits, expert_ref, ext_ref, *refs):
-    meta = ext_ref[:, width:].astype(F32)
-    total = weighted(expert_ref[0], meta, refs[:INNER], top, rows)
+def partial_body(top, rows, width, held, scal_ref, *refs):
+    meta = either(scal_ref, refs[:held], slice(width, None)).astype(F32)
+    refs = refs[held:]
+    total = weighted(scal_ref[0], meta, refs[:INNER], top, rows)
+    for other in refs[INNER:-1]:
+        total = total + other[...].astype(F32)
+    refs[-1][...] = total.astype(BF16)
+
+
+def final_body(top, rows, width, splits, scal_ref, ext_ref, *refs):
+    total = weighted(scal_ref[0], ext_ref[:, width:].astype(F32), refs[:INNER], top, rows)
     others, out = list(refs[INNER:-1]), refs[-1]
     for count in splits:
         pieces = [others.pop(0)[...].astype(F32) for _ in range(count)]
@@ -194,16 +193,27 @@
     return lax.ppermute(array, axis, [(i, i ^ distance) for i in range(lax.axis_size(axis))])
 
 
-def spread(block, outer):
-    if outer != 4:
-        return [(block, block)] + [(got, got) for got in (swap(block, "outer", d) for d in range(1, outer))]
+def relayed(block):
+    def send(array, pairs):
+        return lax.ppermute(array, "outer", pairs)
+
     middle, outward = [(1, 2), (2, 1)], [(1, 0), (2, 3)]
     near = swap(block, "outer", 1)
-    over = lax.ppermute(block, "outer", middle)
-    over_near = lax.ppermute(near, "outer", middle)
-    end_over = lax.ppermute(over, "outer", outward)
-    end_over_near = lax.ppermute(over_near, "outer", outward)
-    return [(block, block), (near, near), (over, end_over), (over_near, end_over_near)]
+    over = send(block, middle)
+    over_near = send(near, middle)
+    end_over = send(over, outward)
+    end_over_near = send(over_near, outward)
+    return [(block,), (near,), (over_near, end_over), (over, end_over_near)]
+
+
+def either(scal_ref, block_refs, columns=slice(None)):
+    if len(block_refs) == 1:
+        return block_refs[0][:, columns]
+    return jnp.where(scal_ref[2] > 0, block_refs[1][:, columns], block_refs[0][:, columns])
+
+
+def lowest(d):
+    return d & -d
 
 
 def column_parts(d, outer):
@@ -240,13 +250,9 @@
 
     move_flops = 2 * tok * INNER * rows * width
     move_bytes = 2 * (tok + INNER * rows) * wide
-    meta = jnp.concatenate(
-        [
-            chosen_expert_index.T.astype(F32),
-            jnp.broadcast_to(token_tenant_index.astype(F32), (8, tok)),
-            router_weight_logits.T,
-        ]
-    )
+    ints = jnp.pad(chosen_expert_index.T, ((0, top + 8), (0, 0)))
+    ints = ints + jnp.pad(token_tenant_index.reshape(1, -1), ((top, top + 7), (0, 0)))
+    meta = ints.astype(F32) + jnp.pad(router_weight_logits.T, ((top + 8, 0), (0, 0)))
     first = pl.pallas_call(
         functools.partial(first_body, top, rows),
         out_shape=[ext_shape] + [packed] * INNER,
@@ -257,7 +263,12 @@
         cost_estimate=pl.CostEstimate(flops=move_flops, bytes_accessed=move_bytes, transcendentals=0),
         name="first",
     )(scal, tokens, meta)
-    blocks = spread(first[0], outer)
+    if outer == 4:
+        blocks = relayed(first[0])
+    else:
+        blocks = [(first[0],)]
+        for d in range(1, outer):
+            blocks.append((swap(blocks[d - lowest(d)][0], "outer", lowest(d)),))
     rows_of = [first[1:]]
 
     ups = [gate_up_weight[0]]
@@ -305,27 +316,25 @@
         got = kernel(scal, adapted[:, 0], *arrived[d], *ups, *downs, *fin, *fup)
         backs.append([[got[i]] + [swap(got[q * parts + i], "inner", q) for q in range(1, INNER)] for i in range(parts)])
 
-    def partial(d, i=0):
-        return call(
-            functools.partial(partial_body, top, rows, width),
-            jax.ShapeDtypeStruct((tok, width // len(backs[d])), BF16),
-            [[scal], *blocks[d], *backs[d][i]],
-            move_flops,
-            move_bytes,
-        )
-
-    if outer == 4:
-        others = []
-        for d, targets in ((2, [(1, 2), (2, 1)]), (3, [(1, 3), (2, 0)])):
-            others.append([])
-            for i in range(len(backs[d])):
-                part = partial(d, i)
-                more = lax.ppermute(part, "outer", [(0, 1), (3, 2)])
-                part = (part.astype(F32) + more.astype(F32)).astype(BF16)
-                others[-1].append(lax.ppermute(part, "outer", targets))
-        others.append([swap(partial(1), "outer", 1)])
-    else:
-        others = [[swap(partial(d), "outer", d)] for d in range(1, outer)]
+    def joining(d, steps):
+        return [[swap(p, "outer", step) for p in partial(d + step)] for step in steps]
+
+    def partial(d):
+        more = joining(d, [1 << bit for bit in range(outer.bit_length()) if 1 << bit < lowest(d)])
+        sums = []
+        for i, rows_back in enumerate(backs[d]):
+            sums.append(
+                call(
+                    functools.partial(partial_body, top, rows, width, len(blocks[d])),
+                    jax.ShapeDtypeStruct((tok, width // len(backs[d])), BF16),
+                    [[scal], *blocks[d], *rows_back, *(m[i] for m in more)],
+                    move_flops,
+                    move_bytes,
+                )
+            )
+        return sums
+
+    others = joining(0, [1 << bit for bit in range(outer.bit_length()) if 1 << bit < outer])
     return call(
         functools.partial(final_body, top, rows, width, [len(other) for other in others]),
         sums,

time: 175 us -> 166 us (0.949)
  starting transfers between devices: 63 us -> 52.9 us
  waiting for transfers between devices: 79.8 us -> 83 us
    ppermute x36 -> x40, waiting for transfers between devices: 54.7 us -> 76.7 us  [swap(): lax.ppermute(array, axis, [(i, i ^ distance) for i in range(lax.axis_size...]
    ppermute x12 -> x4, waiting for transfers between devices: 25.1 us -> 6.27 us  [send(): return lax.ppermute(array, 'outer', pairs)]
    ppermute x12 -> x4, starting transfers between devices: 15.6 us -> 3.94 us  [send(): return lax.ppermute(array, 'outer', pairs)]
    convert_element_type x6 -> x0, other arithmetic: 1.77 us -> none  [the longest x1 0.81 us: shards(): token_tenant_index.astype(F32)]
    ppermute x36 -> x40, starting transfers between devices: 47.4 us -> 48.9 us  [swap(): lax.ppermute(array, axis, [(i, i ^ distance) for i in range(lax.axis_size...]
  transfers between devices with their start and end apart: 48 -> 44, of which waited for: 18 -> 15; matrix products, arithmetic and copies ran while one was open for 0% -> 0% of each run, Pallas kernels for 13% -> 14%
where the time goes in v1:
time: 166 us
  waiting for transfers between devices  83 us (50%)
  starting transfers between devices  52.9 us (32%)
  Pallas kernels  27.7 us (17%)
    ppermute x40, waiting for transfers between devices, swap(): lax.ppermute(array, axis, [(i, i ^ distance) for i in range(lax.axis_size...  76.7 us
    ppermute x40, starting transfers between devices, swap(): lax.ppermute(array, axis, [(i, i ^ distance) for i in range(lax.axis_size...  48.9 us
    pallas_call x9, Pallas kernels, call(): pl.pallas_call(body, out_shape=outs, in_specs=[SMEM] * len(smem) + [VMEM]...  14 us
    pallas_call x4, Pallas kernels, shards(): got = kernel(scal, adapted[:, 0], *arrived[d], *ups, *downs, *fin, *fup)  12.1 us
    ppermute x4, waiting for transfers between devices, send(): return lax.ppermute(array, 'outer', pairs)  6.27 us
    ppermute x4, starting transfers between devices, send(): return lax.ppermute(array, 'outer', pairs)  3.94 us
  transfers between devices with their start and end apart: 44, of which 15 were waited for; matrix products, arithmetic and copies ran while one was open for 0% of the time, Pallas kernels for 14%

profile of v1, /device:TPU:0, one launch (start us, length us, event | category | flops | bytes accessed | tf_op | source)
XLA Modules:
  0.0 165.8 jit_solution(12465050250690961779)
XLA Ops:
  1.9 1.6 first.1
  3.5 3.1 %collective-permute-start.10 = (bf16[128,2176]{1,0:T(8,128)(2,1)S(1)}, bf16[128,2176]{1,0:T(8,128)(2,1)S(1)}, u32[]{:S(2)}, u32[]{:S(2)}) collective-permute-start(bf16[128,2176]{1,0:T(8,128)(2,1)S(1)} %get-tuple-element.46.ext_ref), channel_id=1, source_target_pairs={{0,8},{8,0},{16,24},{24,16},{1,9},{9,1},{17,25},{25,17},{2,10},{10... | collective-permute-start | bytes 1671176 | tf_op jit(solution)/shard_map/ppermute | solution.py:193
  9.4 9.9 %collective-permute-done.10.refs_0_ = bf16[128,2176]{1,0:T(8,128)(2,1)S(1)} collective-permute-done((bf16[128,2176]{1,0:T(8,128)(2,1)S(1)}, bf16[128,2176]{1,0:T(8,128)(2,1)S(1)}, u32[]{:S(2)}, u32[]{:S(2)}) %collective-permute-start.10) | collective-permute-done | bytes 557088 | tf_op jit(solution)/shard_map/ppermute | solution.py:193
  21.9 1.7 %collective-permute-start.1 = (bf16[72,2176]{1,0:T(8,128)(2,1)S(1)}, bf16[72,2176]{1,0:T(8,128)(2,1)S(1)}, u32[]{:S(2)}, u32[]{:S(2)}) collective-permute-start(bf16[72,2176]{1,0:T(8,128)(2,1)S(1)} %get-tuple-element.49), channel_id=1, source_target_pairs={{0,4},{2,6},{4,0},{6,2},{1,5},{3,7},{5,1},{7,3},{8,12},{10,14},{12... | collective-permute-start | bytes 940040 | tf_op jit(solution)/shard_map/ppermute | solution.py:193
  26.4 5.0 %collective-permute-done.1.refs_2_ = bf16[72,2176]{1,0:T(8,128)(2,1)S(1)} collective-permute-done((bf16[72,2176]{1,0:T(8,128)(2,1)S(1)}, bf16[72,2176]{1,0:T(8,128)(2,1)S(1)}, u32[]{:S(2)}, u32[]{:S(2)}) %collective-permute-start.1) | collective-permute-done | bytes 313376 | tf_op jit(solution)/shard_map/ppermute | solution.py:193
  31.4 1.7 %collective-permute-start.11 = (bf16[72,2176]{1,0:T(8,128)(2,1)S(1)}, bf16[72,2176]{1,0:T(8,128)(2,1)S(1)}, u32[]{:S(2)}, u32[]{:S(2)}) collective-permute-start(bf16[72,2176]{1,0:T(8,128)(2,1)S(1)} %get-tuple-element.56), channel_id=1, source_target_pairs={{0,2},{2,0},{4,6},{6,4},{1,3},{3,1},{5,7},{7,5},{8,10},{10,8},{12,... | collective-permute-start | bytes 940040 | tf_op jit(solution)/shard_map/ppermute | solution.py:193
  33.1 6.3 %collective-permute-done.20.refs_1_ = bf16[128,2176]{1,0:T(8,128)(2,1)S(1)} collective-permute-done((bf16[128,2176]{1,0:T(8,128)(2,1)S(1)}, bf16[128,2176]{1,0:T(8,128)(2,1)S(1)}, u32[]{:S(2)}, u32[]{:S(2)}) %collective-permute-start.20) | collective-permute-done | bytes 557088 | tf_op jit(solution)/shard_map/ppermute | solution.py:198
  39.3 1.5 collective-permute-start.12
  44.4 10.7 %collective-permute-done.12.refs_2_ = bf16[72,2176]{1,0:T(8,128)(2,1)S(1)} collective-permute-done((bf16[72,2176]{1,0:T(8,128)(2,1)S(1)}, bf16[72,2176]{1,0:T(8,128)(2,1)S(1)}, u32[]{:S(2)}, u32[]{:S(2)}) %collective-permute-start.12) | collective-permute-done | bytes 313376 | tf_op jit(solution)/shard_map/ppermute | solution.py:193
  55.0 1.5 collective-permute-start.22
  61.6 10.5 %collective-permute-done.22.refs_2_ = bf16[72,2176]{1,0:T(8,128)(2,1)S(1)} collective-permute-done((bf16[72,2176]{1,0:T(8,128)(2,1)S(1)}, bf16[72,2176]{1,0:T(8,128)(2,1)S(1)}, u32[]{:S(2)}, u32[]{:S(2)}) %collective-permute-start.22) | collective-permute-done | bytes 313376 | tf_op jit(solution)/shard_map/ppermute | solution.py:193
  72.1 1.6 collective-permute-start.30
  75.1 3.0 %expert.5 = (bf16[72,2048]{1,0:T(8,128)(2,1)S(1)}, bf16[72,2048]{1,0:T(8,128)(2,1)S(1)}, bf16[72,2048]{1,0:T(8,128)(2,1)S(1)}, bf16[72,2048]{1,0:T(8,128)(2,1)S(1)}) custom-call(s32[3]{0:T(128)S(1)} %pad_add_fusion.1.expert_ref.scal_ref, s32[2]{0:T(128)S(1)} %bitcast.31, bf16[72,2176]{1,0:T(8,128)(2,1)S(1)} %get-tuple-element.55.refs_0_, ...), custom_call_target="tpu_custom_call" | custom-call | flops 1358954496 | bytes 4718592 | tf_op jit(solution)/shard_map/expert/pallas_call | solution.py:316
  78.1 2.1 %collective-permute-start.14 = (bf16[72,2048]{1,0:T(8,128)(2,1)S(1)}, bf16[72,2048]{1,0:T(8,128)(2,1)S(1)}, u32[]{:S(2)}, u32[]{:S(2)}) collective-permute-start(bf16[72,2048]{1,0:T(8,128)(2,1)S(1)} %get-tuple-element.60), channel_id=1, source_target_pairs={{0,2},{2,0},{4,6},{6,4},{1,3},{3,1},{5,7},{7,5},{8,10},{10,8},{12,... | collective-permute-start | bytes 884744 | tf_op jit(solution)/shard_map/ppermute | solution.py:193
  80.2 3.0 %expert.6 = (bf16[72,1024]{1,0:T(8,128)(2,1)S(1)}, bf16[72,1024]{1,0:T(8,128)(2,1)S(1)}, bf16[72,1024]{1,0:T(8,128)(2,1)S(1)}, bf16[72,1024]{1,0:T(8,128)(2,1)S(...) custom-call(s32[3]{0:T(128)S(1)} %pad_add_fusion.1.expert_ref.scal_r, ...), custom_call_target="tpu_custom_call" | custom-call | flops 1358954496 | bytes 4718592 | tf_op jit(solution)/shard_map/expert/pallas_call | solution.py:316
  83.4 6.7 %collective-permute-done.29.refs_2_ = bf16[72,2176]{1,0:T(8,128)(2,1)S(1)} collective-permute-done((bf16[72,2176]{1,0:T(8,128)(2,1)S(1)}, bf16[72,2176]{1,0:T(8,128)(2,1)S(1)}, u32[]{:S(2)}, u32[]{:S(2)}) %collective-permute-start.29) | collective-permute-done | bytes 313376 | tf_op jit(solution)/shard_map/ppermute | solution.py:193
  90.0 1.5 collective-permute-start.25
  92.5 3.0 %expert.7 = (bf16[72,1024]{1,0:T(8,128)(2,1)S(1)}, bf16[72,1024]{1,0:T(8,128)(2,1)S(1)}, bf16[72,1024]{1,0:T(8,128)(2,1)S(1)}, bf16[72,1024]{1,0:T(8,128)(2,1)S(...) custom-call(s32[3]{0:T(128)S(1)} %pad_add_fusion.1.expert_ref.scal_r, ...), custom_call_target="tpu_custom_call" | custom-call | flops 1358954496 | bytes 4718592 | tf_op jit(solution)/shard_map/expert/pallas_call | solution.py:316
  95.5 2.1 %collective-permute-start.15 = (bf16[72,2048]{1,0:T(8,128)(2,1)S(1)}, bf16[72,2048]{1,0:T(8,128)(2,1)S(1)}, u32[]{:S(2)}, u32[]{:S(2)}) collective-permute-start(bf16[72,2048]{1,0:T(8,128)(2,1)S(1)} %get-tuple-element.61), channel_id=1, source_target_pairs={{0,4},{2,6},{4,0},{6,2},{1,5},{3,7},{5,1},{7,3},{8,12},{10,14},{12... | collective-permute-start | bytes 884744 | tf_op jit(solution)/shard_map/ppermute | solution.py:193
  99.5 3.1 %collective-permute-start.41 = (bf16[72,1024]{1,0:T(8,128)(2,1)S(1)}, bf16[72,1024]{1,0:T(8,128)(2,1)S(1)}, u32[]{:S(2)}, u32[]{:S(2)}) collective-permute-start(bf16[72,1024]{1,0:T(8,128)(2,1)S(1)} %get-tuple-element.86), channel_id=1, source_target_pairs={{0,6},{2,4},{4,2},{6,0},{1,7},{3,5},{5,3},{7,1},{8,14},{10,12},{12... | collective-permute-start | bytes 442376 | tf_op jit(solution)/shard_map/ppermute | solution.py:193
  102.5 1.8 %collective-permute-done.39.refs_3_ = bf16[72,1024]{1,0:T(8,128)(2,1)S(1)} collective-permute-done((bf16[72,1024]{1,0:T(8,128)(2,1)S(1)}, bf16[72,1024]{1,0:T(8,128)(2,1)S(1)}, u32[]{:S(2)}, u32[]{:S(2)}) %collective-permute-start.39) | collective-permute-done | bytes 147488 | tf_op jit(solution)/shard_map/ppermute | solution.py:193
  105.1 11.9 %collective-permute-done.40.refs_4_ = bf16[72,1024]{1,0:T(8,128)(2,1)S(1)} collective-permute-done((bf16[72,1024]{1,0:T(8,128)(2,1)S(1)}, bf16[72,1024]{1,0:T(8,128)(2,1)S(1)}, u32[]{:S(2)}, u32[]{:S(2)}) %collective-permute-start.40) | collective-permute-done | bytes 147488 | tf_op jit(solution)/shard_map/ppermute | solution.py:193
  123.2 2.1 %collective-permute-done.32.refs_4_ = bf16[72,1024]{1,0:T(8,128)(2,1)S(1)} collective-permute-done((bf16[72,1024]{1,0:T(8,128)(2,1)S(1)}, bf16[72,1024]{1,0:T(8,128)(2,1)S(1)}, u32[]{:S(2)}, u32[]{:S(2)}) %collective-permute-start.32) | collective-permute-done | bytes 147488 | tf_op jit(solution)/shard_map/ppermute | solution.py:193
  126.3 3.0 %expert.4 = (bf16[72,2048]{1,0:T(8,128)(2,1)S(1)}, bf16[72,2048]{1,0:T(8,128)(2,1)S(1)}, bf16[72,2048]{1,0:T(8,128)(2,1)S(1)}, bf16[72,2048]{1,0:T(8,128)(2,1)S(1)}) custom-call(s32[3]{0:T(128)S(1)} %pad_add_fusion.1.expert_ref.scal_ref, s32[2]{0:T(128)S(1)} %bitcast.34, bf16[72,2176]{1,0:T(8,128)(2,1)S(1)} %get-tuple-element.47.refs_0_, ...), custom_call_target="tpu_custom_call" | custom-call | flops 1358954496 | bytes 4718592 | tf_op jit(solution)/shard_map/expert/pallas_call | solution.py:316
  132.1 1.8 %shard_map.92 = bf16[128,2048]{1,0:T(8,128)(2,1)S(1)} custom-call(s32[3]{0:T(128)S(1)} %pad_add_fusion.1.expert_ref.scal_ref, bf16[128,2176]{1,0:T(8,128)(2,1)S(1)} %collective-permute-done.10.refs_0_, bf16[72,2048]{1,0:T(8,128)(2,1)S(1)} %get-tuple-element.59.refs_1_, bf16[72,2048]{1,0:T(8,128)(2,1)S(1)} %collective-permute-done.14.refs_2_, ...), custom_call_target="tpu_custom_call" | custom-call | flops 150994944 | bytes 1810432 | tf_op jit(solution)/shard_map/pallas_call | solution.py:21
  133.9 2.1 %collective-permute-start.17 = (bf16[128,2048]{1,0:T(8,128)(2,1)S(1)}, bf16[128,2048]{1,0:T(8,128)(2,1)S(1)}, u32[]{:S(2)}, u32[]{:S(2)}) collective-permute-start(bf16[128,2048]{1,0:T(8,128)(2,1)S(1)} %shard_map.92), channel_id=1, source_target_pairs={{0,8},{8,0},{16,24},{24,16},{1,9},{9,1},{17,25},{25,17},{2,10},{10... | collective-permute-start | bytes 1572872 | tf_op jit(solution)/shard_map/ppermute | solution.py:193
  137.3 6.1 %collective-permute-done.38.refs_5_ = bf16[72,1024]{1,0:T(8,128)(2,1)S(1)} collective-permute-done((bf16[72,1024]{1,0:T(8,128)(2,1)S(1)}, bf16[72,1024]{1,0:T(8,128)(2,1)S(1)}, u32[]{:S(2)}, u32[]{:S(2)}) %collective-permute-start.38) | collective-permute-done | bytes 147488 | tf_op jit(solution)/shard_map/ppermute | solution.py:193
  148.6 3.0 %collective-permute-start.35 = (bf16[128,1024]{1,0:T(8,128)(2,1)S(1)}, bf16[128,1024]{1,0:T(8,128)(2,1)S(1)}, u32[]{:S(2)}, u32[]{:S(2)}) collective-permute-start(bf16[128,1024]{1,0:T(8,128)(2,1)S(1)} %shard_map.96), channel_id=1, source_target_pairs={{0,16},{8,24},{16,0},{24,8},{1,17},{9,25},{17,1},{25,9},{2,18},{10... | collective-permute-start | bytes 786440 | tf_op jit(solution)/shard_map/ppermute | solution.py:193
  151.6 1.8 %collective-permute-done.8.refs_2_ = bf16[72,2048]{1,0:T(8,128)(2,1)S(1)} collective-permute-done((bf16[72,2048]{1,0:T(8,128)(2,1)S(1)}, bf16[72,2048]{1,0:T(8,128)(2,1)S(1)}, u32[]{:S(2)}, u32[]{:S(2)}) %collective-permute-start.8) | collective-permute-done | bytes 294944 | tf_op jit(solution)/shard_map/ppermute | solution.py:193
  153.3 7.1 %collective-permute-done.43.refs_6_ = bf16[128,1024]{1,0:T(8,128)(2,1)S(1)} collective-permute-done((bf16[128,1024]{1,0:T(8,128)(2,1)S(1)}, bf16[128,1024]{1,0:T(8,128)(2,1)S(1)}, u32[]{:S(2)}, u32[]{:S(2)}) %collective-permute-start.43) | collective-permute-done | bytes 262176 | tf_op jit(solution)/shard_map/ppermute | solution.py:193
  160.5 2.8 %collective-permute-done.35.refs_5_ = bf16[128,1024]{1,0:T(8,128)(2,1)S(1)} collective-permute-done((bf16[128,1024]{1,0:T(8,128)(2,1)S(1)}, bf16[128,1024]{1,0:T(8,128)(2,1)S(1)}, u32[]{:S(2)}, u32[]{:S(2)}) %collective-permute-start.35) | collective-permute-done | bytes 262176 | tf_op jit(solution)/shard_map/ppermute | solution.py:193
  163.3 2.5 %shard_map.99 = bf16[128,2048]{1,0:T(8,128)(2,1)} custom-call(s32[3]{0:T(128)S(1)} %pad_add_fusion.1.expert_ref.scal_ref, bf16[128,2176]{1,0:T(8,128)(2,1)S(1)} %get-tuple-element.46.ext_ref, bf16[72,2048]{1,0:T(8,128)(2,1)S(1)} %get-tuple-element.51.refs_0_, bf16[72,2048]{1,0:T(8,128)(2,1)S(1)} %collective-permute-done.7.refs_1_, ...), custom_call_target="tpu_custom_call" | custom-call | flops 150994944 | bytes 1810432 | tf_op jit(solution)/shard_map/pallas_call | solution.py:21
  (84 shorter events, 39.9 us)
Async XLA Ops:
  3.5 15.7 %collective-permute-start.10 = (bf16[128,2176]{1,0:T(8,128)(2,1)S(1)}, bf16[128,2176]{1,0:T(8,128)(2,1)S(1)}, u32[]{:S(2)}, u32[]{:S(2)}) collective-permute-start(bf16[128,2176]{1,0:T(8,128)(2,1)S(1)} %get-tuple-element.46.ext_ref), channel_id=1, source_target_pairs={{0,8},{8,0},{16,24},{24,16},{1,9},{9,1},{17,25},{25,17},{2,10},{10... | collective-permute-start | bytes 1671176 | tf_op jit(solution)/shard_map/ppermute | solution.py:193
  6.6 13.4 %collective-permute-start.19 = (bf16[128,2176]{1,0:T(8,128)(2,1)S(1)}, bf16[128,2176]{1,0:T(8,128)(2,1)S(1)}, u32[]{:S(2)}, u32[]{:S(2)}) collective-permute-start(bf16[128,2176]{1,0:T(8,128)(2,1)S(1)} %get-tuple-element.46.ext_ref), channel_id=1, source_target_pairs={{8,16},{16,8},{9,17},{17,9},{10,18},{18,10},{11,19},{19,11},{12,20... | collective-permute-start | bytes 1671176 | tf_op jit(solution)/shard_map/ppermute | solution.py:198
  7.3 66.4 %collective-permute-start.3 = (bf16[1024,768]{1,0:T(8,128)(2,1)}, bf16[1024,768]{1,0:T(8,128)(2,1)S(1)}, u32[]{:S(2)}, u32[]{:S(2)}) collective-permute-start(bf16[1024,768]{1,0:T(8,128)(2,1)} %bitcast.11), channel_id=1, source_target_pairs={{0,1},{1,0},{2,3},{3,2},{4,5},{5,4},{6,7},{7,6},{8,9},{9,8},{10,11... | collective-permute-start | bytes 4718600 | tf_op jit(solution)/shard_map/ppermute | solution.py:193
  7.4 12.5 %collective-permute-start.6 = (bf16[32,384]{1,0:T(8,128)(2,1)}, bf16[32,384]{1,0:T(8,128)(2,1)S(1)}, u32[]{:S(2)}, u32[]{:S(2)}) collective-permute-start(bf16[32,384]{1,0:T(8,128)(2,1)} %bitcast.26), channel_id=1, source_target_pairs={{0,1},{1,0},{2,3},{3,2},{4,5},{5,4},{6,7},{7,6},{8,9},{9,8},{10,11... | collective-permute-start | bytes 73736 | tf_op jit(solution)/shard_map/ppermute | solution.py:193
  7.9 14.0 %collective-permute-start = (bf16[72,2176]{1,0:T(8,128)(2,1)S(1)}, bf16[72,2176]{1,0:T(8,128)(2,1)S(1)}, u32[]{:S(2)}, u32[]{:S(2)}) collective-permute-start(bf16[72,2176]{1,0:T(8,128)(2,1)S(1)} %get-tuple-element.48), channel_id=1, source_target_pairs={{0,2},{2,0},{4,6},{6,4},{1,3},{3,1},{5,7},{7,5},{8,10},{10,8},{12,... | collective-permute-start | bytes 940040 | tf_op jit(solution)/shard_map/ppermute | solution.py:193
  20.1 19.3 %collective-permute-start.20 = (bf16[128,2176]{1,0:T(8,128)(2,1)S(1)}, bf16[128,2176]{1,0:T(8,128)(2,1)S(1)}, u32[]{:S(2)}, u32[]{:S(2)}) collective-permute-start(bf16[128,2176]{1,0:T(8,128)(2,1)S(1)} %collective-permute-done.19.refs_0_), channel_id=1, source_target_pairs={{8,0},{16,24},{9,1},{17,25},{10,2},{18,26},{11,3},{19,27},{12,4},{... | collective-permute-start | bytes 1671176 | tf_op jit(solution)/shard_map/ppermute | solution.py:198
  21.6 20.8 %collective-permute-start.4 = (bf16[384,1024]{1,0:T(8,128)(2,1)}, bf16[384,1024]{1,0:T(8,128)(2,1)S(1)}, u32[]{:S(2)}, u32[]{:S(2)}) collective-permute-start(bf16[384,1024]{1,0:T(8,128)(2,1)} %bitcast.16), channel_id=1, source_target_pairs={{0,1},{1,0},{2,3},{3,2},{4,5},{5,4},{6,7},{7,6},{8,9},{9,8},{10,11... | collective-permute-start | bytes 2359304 | tf_op jit(solution)/shard_map/ppermute | solution.py:193
  23.6 33.0 %collective-permute-start.27 = (bf16[128,2176]{1,0:T(8,128)(2,1)S(1)}, bf16[128,2176]{1,0:T(8,128)(2,1)S(1)}, u32[]{:S(2)}, u32[]{:S(2)}) collective-permute-start(bf16[128,2176]{1,0:T(8,128)(2,1)S(1)} %collective-permute-done.18.refs_0_), channel_id=1, source_target_pairs={{8,0},{16,24},{9,1},{17,25},{10,2},{18,26},{11,3},{19,27},{12,4},{... | collective-permute-start | bytes 1671176 | tf_op jit(solution)/shard_map/ppermute | solution.py:198
  39.3 15.7 %collective-permute-start.12 = (bf16[72,2176]{1,0:T(8,128)(2,1)S(1)}, bf16[72,2176]{1,0:T(8,128)(2,1)S(1)}, u32[]{:S(2)}, u32[]{:S(2)}) collective-permute-start(bf16[72,2176]{1,0:T(8,128)(2,1)S(1)} %get-tuple-element.57), channel_id=1, source_target_pairs={{0,4},{2,6},{4,0},{6,2},{1,5},{3,7},{5,1},{7,3},{8,12},{10,14},{12... | collective-permute-start | bytes 940040 | tf_op jit(solution)/shard_map/ppermute | solution.py:193
  42.4 17.1 %collective-permute-start.13 = (bf16[72,2176]{1,0:T(8,128)(2,1)S(1)}, bf16[72,2176]{1,0:T(8,128)(2,1)S(1)}, u32[]{:S(2)}, u32[]{:S(2)}) collective-permute-start(bf16[72,2176]{1,0:T(8,128)(2,1)S(1)} %get-tuple-element.58), channel_id=1, source_target_pairs={{0,6},{2,4},{4,2},{6,0},{1,7},{3,5},{5,3},{7,1},{8,14},{10,12},{12... | collective-permute-start | bytes 940040 | tf_op jit(solution)/shard_map/ppermute | solution.py:193
  43.9 16.3 %collective-permute-start.21 = (bf16[72,2176]{1,0:T(8,128)(2,1)S(1)}, bf16[72,2176]{1,0:T(8,128)(2,1)S(1)}, u32[]{:S(2)}, u32[]{:S(2)}) collective-permute-start(bf16[72,2176]{1,0:T(8,128)(2,1)S(1)} %get-tuple-element.64), channel_id=1, source_target_pairs={{0,2},{2,0},{4,6},{6,4},{1,3},{3,1},{5,7},{7,5},{8,10},{10,8},{12,... | collective-permute-start | bytes 940040 | tf_op jit(solution)/shard_map/ppermute | solution.py:193
  55.0 17.1 %collective-permute-start.22 = (bf16[72,2176]{1,0:T(8,128)(2,1)S(1)}, bf16[72,2176]{1,0:T(8,128)(2,1)S(1)}, u32[]{:S(2)}, u32[]{:S(2)}) collective-permute-start(bf16[72,2176]{1,0:T(8,128)(2,1)S(1)} %get-tuple-element.65), channel_id=1, source_target_pairs={{0,4},{2,6},{4,0},{6,2},{1,5},{3,7},{5,1},{7,3},{8,12},{10,14},{12... | collective-permute-start | bytes 940040 | tf_op jit(solution)/shard_map/ppermute | solution.py:193
  56.6 21.6 %collective-permute-start.23 = (bf16[72,2176]{1,0:T(8,128)(2,1)S(1)}, bf16[72,2176]{1,0:T(8,128)(2,1)S(1)}, u32[]{:S(2)}, u32[]{:S(2)}) collective-permute-start(bf16[72,2176]{1,0:T(8,128)(2,1)S(1)} %get-tuple-element.66), channel_id=1, source_target_pairs={{0,6},{2,4},{4,2},{6,0},{1,7},{3,5},{5,3},{7,1},{8,14},{10,12},{12... | collective-permute-start | bytes 940040 | tf_op jit(solution)/shard_map/ppermute | solution.py:193
  59.5 23.8 %collective-permute-start.28 = (bf16[72,2176]{1,0:T(8,128)(2,1)S(1)}, bf16[72,2176]{1,0:T(8,128)(2,1)S(1)}, u32[]{:S(2)}, u32[]{:S(2)}) collective-permute-start(bf16[72,2176]{1,0:T(8,128)(2,1)S(1)} %get-tuple-element.72), channel_id=1, source_target_pairs={{0,2},{2,0},{4,6},{6,4},{1,3},{3,1},{5,7},{7,5},{8,10},{10,8},{12,... | collective-permute-start | bytes 940040 | tf_op jit(solution)/shard_map/ppermute | solution.py:193
  60.1 29.9 %collective-permute-start.29 = (bf16[72,2176]{1,0:T(8,128)(2,1)S(1)}, bf16[72,2176]{1,0:T(8,128)(2,1)S(1)}, u32[]{:S(2)}, u32[]{:S(2)}) collective-permute-start(bf16[72,2176]{1,0:T(8,128)(2,1)S(1)} %get-tuple-element.73), channel_id=1, source_target_pairs={{0,4},{2,6},{4,0},{6,2},{1,5},{3,7},{5,1},{7,3},{8,12},{10,14},{12... | collective-permute-start | bytes 940040 | tf_op jit(solution)/shard_map/ppermute | solution.py:193
  72.1 19.4 %collective-permute-start.30 = (bf16[72,2176]{1,0:T(8,128)(2,1)S(1)}, bf16[72,2176]{1,0:T(8,128)(2,1)S(1)}, u32[]{:S(2)}, u32[]{:S(2)}) collective-permute-start(bf16[72,2176]{1,0:T(8,128)(2,1)S(1)} %get-tuple-element.74), channel_id=1, source_target_pairs={{0,6},{2,4},{4,2},{6,0},{1,7},{3,5},{5,3},{7,1},{8,14},{10,12},{12... | collective-permute-start | bytes 940040 | tf_op jit(solution)/shard_map/ppermute | solution.py:193
  73.8 21.8 %collective-permute-start.2 = (bf16[72,2176]{1,0:T(8,128)(2,1)S(1)}, bf16[72,2176]{1,0:T(8,128)(2,1)S(1)}, u32[]{:S(2)}, u32[]{:S(2)}) collective-permute-start(bf16[72,2176]{1,0:T(8,128)(2,1)S(1)} %get-tuple-element.50), channel_id=1, source_target_pairs={{0,6},{2,4},{4,2},{6,0},{1,7},{3,5},{5,3},{7,1},{8,14},{10,12},{12... | collective-permute-start | bytes 940040 | tf_op jit(solution)/shard_map/ppermute | solution.py:193
  78.1 24.4 %collective-permute-start.14 = (bf16[72,2048]{1,0:T(8,128)(2,1)S(1)}, bf16[72,2048]{1,0:T(8,128)(2,1)S(1)}, u32[]{:S(2)}, u32[]{:S(2)}) collective-permute-start(bf16[72,2048]{1,0:T(8,128)(2,1)S(1)} %get-tuple-element.60), channel_id=1, source_target_pairs={{0,2},{2,0},{4,6},{6,4},{1,3},{3,1},{5,7},{7,5},{8,10},{10,8},{12,... | collective-permute-start | bytes 884744 | tf_op jit(solution)/shard_map/ppermute | solution.py:193
  83.3 14.3 %collective-permute-start.24 = (bf16[72,1024]{1,0:T(8,128)(2,1)S(1)}, bf16[72,1024]{1,0:T(8,128)(2,1)S(1)}, u32[]{:S(2)}, u32[]{:S(2)}) collective-permute-start(bf16[72,1024]{1,0:T(8,128)(2,1)S(1)} %get-tuple-element.68), channel_id=1, source_target_pairs={{0,2},{2,0},{4,6},{6,4},{1,3},{3,1},{5,7},{7,5},{8,10},{10,8},{12,... | collective-permute-start | bytes 442376 | tf_op jit(solution)/shard_map/ppermute | solution.py:193
  95.5 25.5 %collective-permute-start.15 = (bf16[72,2048]{1,0:T(8,128)(2,1)S(1)}, bf16[72,2048]{1,0:T(8,128)(2,1)S(1)}, u32[]{:S(2)}, u32[]{:S(2)}) collective-permute-start(bf16[72,2048]{1,0:T(8,128)(2,1)S(1)} %get-tuple-element.61), channel_id=1, source_target_pairs={{0,4},{2,6},{4,0},{6,2},{1,5},{3,7},{5,1},{7,3},{8,12},{10,14},{12... | collective-permute-start | bytes 884744 | tf_op jit(solution)/shard_map/ppermute | solution.py:193
  98.4 18.6 %collective-permute-start.40 = (bf16[72,1024]{1,0:T(8,128)(2,1)S(1)}, bf16[72,1024]{1,0:T(8,128)(2,1)S(1)}, u32[]{:S(2)}, u32[]{:S(2)}) collective-permute-start(bf16[72,1024]{1,0:T(8,128)(2,1)S(1)} %get-tuple-element.85), channel_id=1, source_target_pairs={{0,4},{2,6},{4,0},{6,2},{1,5},{3,7},{5,1},{7,3},{8,12},{10,14},{12... | collective-permute-start | bytes 442376 | tf_op jit(solution)/shard_map/ppermute | solution.py:193
  99.5 18.9 %collective-permute-start.41 = (bf16[72,1024]{1,0:T(8,128)(2,1)S(1)}, bf16[72,1024]{1,0:T(8,128)(2,1)S(1)}, u32[]{:S(2)}, u32[]{:S(2)}) collective-permute-start(bf16[72,1024]{1,0:T(8,128)(2,1)S(1)} %get-tuple-element.86), channel_id=1, source_target_pairs={{0,6},{2,4},{4,2},{6,0},{1,7},{3,5},{5,3},{7,1},{8,14},{10,12},{12... | collective-permute-start | bytes 442376 | tf_op jit(solution)/shard_map/ppermute | solution.py:193
  102.5 29.5 %collective-permute-start.16 = (bf16[72,2048]{1,0:T(8,128)(2,1)S(1)}, bf16[72,2048]{1,0:T(8,128)(2,1)S(1)}, u32[]{:S(2)}, u32[]{:S(2)}) collective-permute-start(bf16[72,2048]{1,0:T(8,128)(2,1)S(1)} %get-tuple-element.62), channel_id=1, source_target_pairs={{0,6},{2,4},{4,2},{6,0},{1,7},{3,5},{5,3},{7,1},{8,14},{10,12},{12... | collective-permute-start | bytes 884744 | tf_op jit(solution)/shard_map/ppermute | solution.py:193
  104.4 17.5 %collective-permute-start.31 = (bf16[72,1024]{1,0:T(8,128)(2,1)S(1)}, bf16[72,1024]{1,0:T(8,128)(2,1)S(1)}, u32[]{:S(2)}, u32[]{:S(2)}) collective-permute-start(bf16[72,1024]{1,0:T(8,128)(2,1)S(1)} %get-tuple-element.76), channel_id=1, source_target_pairs={{0,2},{2,0},{4,6},{6,4},{1,3},{3,1},{5,7},{7,5},{8,10},{10,8},{12,... | collective-permute-start | bytes 442376 | tf_op jit(solution)/shard_map/ppermute | solution.py:193
  121.0 12.9 %collective-permute-start.36 = (bf16[72,1024]{1,0:T(8,128)(2,1)S(1)}, bf16[72,1024]{1,0:T(8,128)(2,1)S(1)}, u32[]{:S(2)}, u32[]{:S(2)}) collective-permute-start(bf16[72,1024]{1,0:T(8,128)(2,1)S(1)} %get-tuple-element.80), channel_id=1, source_target_pairs={{0,2},{2,0},{4,6},{6,4},{1,3},{3,1},{5,7},{7,5},{8,10},{10,8},{12,... | collective-permute-start | bytes 442376 | tf_op jit(solution)/shard_map/ppermute | solution.py:193
  121.8 14.2 %collective-permute-start.37 = (bf16[72,1024]{1,0:T(8,128)(2,1)S(1)}, bf16[72,1024]{1,0:T(8,128)(2,1)S(1)}, u32[]{:S(2)}, u32[]{:S(2)}) collective-permute-start(bf16[72,1024]{1,0:T(8,128)(2,1)S(1)} %get-tuple-element.81), channel_id=1, source_target_pairs={{0,4},{2,6},{4,0},{6,2},{1,5},{3,7},{5,1},{7,3},{8,12},{10,14},{12... | collective-permute-start | bytes 442376 | tf_op jit(solution)/shard_map/ppermute | solution.py:193
  125.3 19.0 %collective-permute-start.42 = (bf16[128,1024]{1,0:T(8,128)(2,1)S(1)}, bf16[128,1024]{1,0:T(8,128)(2,1)S(1)}, u32[]{:S(2)}, u32[]{:S(2)}) collective-permute-start(bf16[128,1024]{1,0:T(8,128)(2,1)S(1)} %shard_map.97), channel_id=1, source_target_pairs={{0,8},{8,0},{16,24},{24,16},{1,9},{9,1},{17,25},{25,17},{2,10},{10... | collective-permute-start | bytes 786440 | tf_op jit(solution)/shard_map/ppermute | solution.py:193
  129.3 19.2 %collective-permute-start.7 = (bf16[72,2048]{1,0:T(8,128)(2,1)S(1)}, bf16[72,2048]{1,0:T(8,128)(2,1)S(1)}, u32[]{:S(2)}, u32[]{:S(2)}) collective-permute-start(bf16[72,2048]{1,0:T(8,128)(2,1)S(1)} %get-tuple-element.52), channel_id=1, source_target_pairs={{0,2},{2,0},{4,6},{6,4},{1,3},{3,1},{5,7},{7,5},{8,10},{10,8},{12,... | collective-permute-start | bytes 884744 | tf_op jit(solution)/shard_map/ppermute | solution.py:193
  132.1 15.1 %collective-permute-start.34 = (bf16[128,1024]{1,0:T(8,128)(2,1)S(1)}, bf16[128,1024]{1,0:T(8,128)(2,1)S(1)}, u32[]{:S(2)}, u32[]{:S(2)}) collective-permute-start(bf16[128,1024]{1,0:T(8,128)(2,1)S(1)} %shard_map.95), channel_id=1, source_target_pairs={{0,8},{8,0},{16,24},{24,16},{1,9},{9,1},{17,25},{25,17},{2,10},{10... | collective-permute-start | bytes 786440 | tf_op jit(solution)/shard_map/ppermute | solution.py:193
  133.9 19.4 %collective-permute-start.17 = (bf16[128,2048]{1,0:T(8,128)(2,1)S(1)}, bf16[128,2048]{1,0:T(8,128)(2,1)S(1)}, u32[]{:S(2)}, u32[]{:S(2)}) collective-permute-start(bf16[128,2048]{1,0:T(8,128)(2,1)S(1)} %shard_map.92), channel_id=1, source_target_pairs={{0,8},{8,0},{16,24},{24,16},{1,9},{9,1},{17,25},{25,17},{2,10},{10... | collective-permute-start | bytes 1572872 | tf_op jit(solution)/shard_map/ppermute | solution.py:193
  147.2 13.3 %collective-permute-start.43 = (bf16[128,1024]{1,0:T(8,128)(2,1)S(1)}, bf16[128,1024]{1,0:T(8,128)(2,1)S(1)}, u32[]{:S(2)}, u32[]{:S(2)}) collective-permute-start(bf16[128,1024]{1,0:T(8,128)(2,1)S(1)} %shard_map.98), channel_id=1, source_target_pairs={{0,16},{8,24},{16,0},{24,8},{1,17},{9,25},{17,1},{25,9},{2,18},{10... | collective-permute-start | bytes 786440 | tf_op jit(solution)/shard_map/ppermute | solution.py:193
  148.6 14.7 %collective-permute-start.35 = (bf16[128,1024]{1,0:T(8,128)(2,1)S(1)}, bf16[128,1024]{1,0:T(8,128)(2,1)S(1)}, u32[]{:S(2)}, u32[]{:S(2)}) collective-permute-start(bf16[128,1024]{1,0:T(8,128)(2,1)S(1)} %shard_map.96), channel_id=1, source_target_pairs={{0,16},{8,24},{16,0},{24,8},{1,17},{9,25},{17,1},{25,9},{2,18},{10... | collective-permute-start | bytes 786440 | tf_op jit(solution)/shard_map/ppermute | solution.py:193
  (18 other events, 463.7 us)

commit v2 on v1

--- a/solution.py
+++ b/solution.py
@@ -62,11 +62,18 @@
     return picked.astype(BF16)
 
 
-def pack_rows(slots, wide, outs, rows):
-    picked = one_hot(slots, rows)
-    got = lax.dot_general(picked, wide, (((0,), (0,)), ((), ())), preferred_element_type=F32).astype(BF16)
-    for q in range(INNER):
-        outs[q][...] = got[q * rows : (q + 1) * rows]
+def pack_rows(slots, wide, meta_t, outs, top, rows):
+    tok, width = wide.shape[0], wide.shape[1] - LANES
+    got = lax.dot_general(
+        one_hot(slots, rows), wide[:, :width], (((0,), (0,)), ((), ())), preferred_element_type=F32
+    ).astype(BF16)
+    tenant = meta_t[top : top + 8].astype(BF16)
+    lane = iota((tok, LANES), 1).astype(F32)
+    for q in range(INNER):
+        for c in range(width // LANES):
+            outs[q][c * rows : (c + 1) * rows] = got[q * rows : (q + 1) * rows, c * LANES : (c + 1) * LANES]
+        picked = jnp.where(lane == slots[q], 1.0, 0.0).astype(BF16)
+        outs[q][width // LANES * rows :] = jnp.dot(tenant, picked, preferred_element_type=F32).astype(BF16)
 
 
 def first_body(top, rows, expert_ref, tok_any, meta_ref, ext_ref, *refs):
@@ -97,15 +104,16 @@
     ext_ref[:, width:] = meta.astype(BF16)
     slots = packing(meta, expert_ref[0], top)
     copy.wait()
-    pack_rows(slots, ext_ref[...], outs, rows)
+    pack_rows(slots, ext_ref[...], meta_t, outs, top, rows)
 
 
 def pack_body(top, rows, width, scal_ref, *refs):
     wide = either(scal_ref, refs[:-INNER])
-    pack_rows(packing(wide[:, width:].astype(F32), scal_ref[0], top), wide, refs[-INNER:], rows)
-
-
-def expert_body(top, rows, stores, parts, scal_ref, adapted_ref, *refs):
+    meta = wide[:, width:].astype(F32)
+    pack_rows(packing(meta, scal_ref[0], top), wide, meta.T, refs[-INNER:], top, rows)
+
+
+def expert_body(rows, stores, parts, scal_ref, adapted_ref, *refs):
     xs, refs = refs[:INNER], refs[INNER:]
     ups, refs = refs[:stores], refs[stores:]
     downs, refs = refs[:stores], refs[stores:]
@@ -115,8 +123,12 @@
     store = scal_ref[1]
     width = ups[0].shape[0] * stores
     hidden = downs[0].shape[0]
-    for q in range(INNER):
-        x_ref[q * rows : (q + 1) * rows] = xs[q][...]
+    codes = []
+    for q in range(INNER):
+        for c in range(width // LANES):
+            x_ref[q * rows : (q + 1) * rows, c * LANES : (c + 1) * LANES] = xs[q][c * rows : (c + 1) * rows]
+        codes.append(xs[q][width // LANES * rows :].astype(F32).T[:rows, :1])
+    code = jnp.concatenate(codes, axis=0)
     k = ups[0].shape[0]
     pre = None
     for r in range(stores):
@@ -136,9 +148,8 @@
     allowed = jnp.zeros(lane.shape, F32)
     for u in range(tenants):
         allowed = jnp.where(tenant == u, adapted_ref[u].astype(F32), allowed)
-    code = x_ref[:, width + top : width + top + 1].astype(F32)
     low = lax.dot_general(
-        x_ref[:, :width], fin_ref[...], (((1,), (1,)), ((), ())), preferred_element_type=F32
+        x_ref[...], fin_ref[...], (((1,), (1,)), ((), ())), preferred_element_type=F32
     )
     low = (low * jnp.where(code == tenant.astype(F32), allowed, 0.0)).astype(BF16)
     zero = jnp.zeros_like(low)
@@ -244,7 +255,7 @@
     place = lax.axis_index("outer")
     ends = jnp.logical_or(place == 0, place == outer - 1)
     scal = jnp.stack([expert, store, ends.astype(jnp.int32)]).astype(jnp.int32)
-    packed = jax.ShapeDtypeStruct((rows, wide), BF16)
+    packed = jax.ShapeDtypeStruct((width // LANES * rows + 8, LANES), BF16)
     ext_shape = jax.ShapeDtypeStruct((tok, wide), BF16)
     sums = jax.ShapeDtypeStruct((tok, width), BF16)
 
@@ -297,12 +308,12 @@
     for d in range(outer):
         parts = column_parts(d, outer)
         kernel = pl.pallas_call(
-            functools.partial(expert_body, top, rows, stores, parts),
+            functools.partial(expert_body, rows, stores, parts),
             out_shape=[jax.ShapeDtypeStruct((rows, width // parts), BF16)] * (INNER * parts),
             in_specs=[SMEM] * 2 + [VMEM] * (INNER + 4 * stores),
             out_specs=[VMEM] * (INNER * parts),
             scratch_shapes=[
-                pltpu.VMEM((INNER * rows, wide), BF16),
+                pltpu.VMEM((INNER * rows, width), BF16),
                 pltpu.VMEM((stores * fin[0].shape[0], width), BF16),
                 pltpu.VMEM((stores * fin[0].shape[0], hidden), BF16),
                 pltpu.VMEM((INNER * rows, width), BF16),

time: 166 us -> 167 us (level)
  starting transfers between devices: 52.9 us -> 60.8 us
  waiting for transfers between devices: 83 us -> 75.2 us
    ppermute x40, starting transfers between devices: 48.9 us -> 56.9 us  [swap(): lax.ppermute(array, axis, [(i, i ^ distance) for i in range(lax.axis_size...]
    ppermute x4, waiting for transfers between devices: 6.27 us -> 1.4 us  [send(): return lax.ppermute(array, 'outer', pairs)]
    ppermute x40, waiting for transfers between devices: 76.7 us -> 73.8 us  [swap(): lax.ppermute(array, axis, [(i, i ^ distance) for i in range(lax.axis_size...]
  transfers between devices with their start and end apart: 44 -> 44, of which waited for: 15 -> 17; matrix products, arithmetic and copies ran while one was open for 0% -> 0% of each run, Pallas kernels for 14% -> 15%
where the time goes in v2:
time: 167 us
  waiting for transfers between devices  75.2 us (45%)
  starting transfers between devices  60.8 us (36%)
  Pallas kernels  28.3 us (17%)
    ppermute x40, waiting for transfers between devices, swap(): lax.ppermute(array, axis, [(i, i ^ distance) for i in range(lax.axis_size...  73.8 us
    ppermute x40, starting transfers between devices, swap(): lax.ppermute(array, axis, [(i, i ^ distance) for i in range(lax.axis_size...  56.9 us
    pallas_call x9, Pallas kernels, call(): pl.pallas_call(body, out_shape=outs, in_specs=[SMEM] * len(smem) + [VMEM]...  13.8 us
    pallas_call x4, Pallas kernels, shards(): got = kernel(scal, adapted[:, 0], *arrived[d], *ups, *downs, *fin, *fup)  12.9 us
    ppermute x4, starting transfers between devices, send(): return lax.ppermute(array, 'outer', pairs)  3.93 us
  transfers between devices with their start and end apart: 44, of which 17 were waited for; matrix products, arithmetic and copies ran while one was open for 0% of the time, Pallas kernels for 15%

profile of v2, /device:TPU:0, one launch (start us, length us, event | category | flops | bytes accessed | tf_op | source)
XLA Modules:
  0.0 166.5 jit_solution(9985565769910311511)
XLA Ops:
  3.5 3.1 %collective-permute-start.10 = (bf16[128,2176]{1,0:T(8,128)(2,1)S(1)}, bf16[128,2176]{1,0:T(8,128)(2,1)S(1)}, u32[]{:S(2)}, u32[]{:S(2)}) collective-permute-start(bf16[128,2176]{1,0:T(8,128)(2,1)S(1)} %get-tuple-element.46.ext_ref), channel_id=1, source_target_pairs={{0,8},{8,0},{16,24},{24,16},{1,9},{9,1},{17,25},{25,17},{2,10},{10... | collective-permute-start | bytes 1671176 | tf_op jit(solution)/shard_map/ppermute | solution.py:204
  7.4 11.9 %collective-permute-done.10.refs_0_ = bf16[128,2176]{1,0:T(8,128)(2,1)S(1)} collective-permute-done((bf16[128,2176]{1,0:T(8,128)(2,1)S(1)}, bf16[128,2176]{1,0:T(8,128)(2,1)S(1)}, u32[]{:S(2)}, u32[]{:S(2)}) %collective-permute-start.10) | collective-permute-done | bytes 557088 | tf_op jit(solution)/shard_map/ppermute | solution.py:204
  24.7 6.2 %collective-permute-done.refs_1_ = bf16[1160,128]{1,0:T(8,128)(2,1)S(1)} collective-permute-done((bf16[1160,128]{1,0:T(8,128)(2,1)S(1)}, bf16[1160,128]{1,0:T(8,128)(2,1)S(1)}, u32[]{:S(2)}, u32[]{:S(2)}) %collective-permute-start) | collective-permute-done | bytes 296992 | tf_op jit(solution)/shard_map/ppermute | solution.py:204
  30.9 1.7 %collective-permute-start.1 = (bf16[1160,128]{1,0:T(8,128)(2,1)S(1)}, bf16[1160,128]{1,0:T(8,128)(2,1)S(1)}, u32[]{:S(2)}, u32[]{:S(2)}) collective-permute-start(bf16[1160,128]{1,0:T(8,128)(2,1)S(1)} %get-tuple-element.49), channel_id=1, source_target_pairs={{0,4},{2,6},{4,0},{6,2},{1,5},{3,7},{5,1},{7,3},{8,12},{10,14},{12... | collective-permute-start | bytes 890888 | tf_op jit(solution)/shard_map/ppermute | solution.py:204
  35.4 3.9 %collective-permute-done.1.refs_2_ = bf16[1160,128]{1,0:T(8,128)(2,1)S(1)} collective-permute-done((bf16[1160,128]{1,0:T(8,128)(2,1)S(1)}, bf16[1160,128]{1,0:T(8,128)(2,1)S(1)}, u32[]{:S(2)}, u32[]{:S(2)}) %collective-permute-start.1) | collective-permute-done | bytes 296992 | tf_op jit(solution)/shard_map/ppermute | solution.py:204
  47.5 2.5 %collective-permute-start.21 = (bf16[1160,128]{1,0:T(8,128)(2,1)S(1)}, bf16[1160,128]{1,0:T(8,128)(2,1)S(1)}, u32[]{:S(2)}, u32[]{:S(2)}) collective-permute-start(bf16[1160,128]{1,0:T(8,128)(2,1)S(1)} %get-tuple-element.64), channel_id=1, source_target_pairs={{0,2},{2,0},{4,6},{6,4},{1,3},{3,1},{5,7},{7,5},{8,10},{10,8},{12,... | collective-permute-start | bytes 890888 | tf_op jit(solution)/shard_map/ppermute | solution.py:204
  50.0 6.9 %collective-permute-done.12.refs_2_ = bf16[1160,128]{1,0:T(8,128)(2,1)S(1)} collective-permute-done((bf16[1160,128]{1,0:T(8,128)(2,1)S(1)}, bf16[1160,128]{1,0:T(8,128)(2,1)S(1)}, u32[]{:S(2)}, u32[]{:S(2)}) %collective-permute-start.12) | collective-permute-done | bytes 296992 | tf_op jit(solution)/shard_map/ppermute | solution.py:204
  58.4 1.7 %collective-permute-start.23 = (bf16[1160,128]{1,0:T(8,128)(2,1)S(1)}, bf16[1160,128]{1,0:T(8,128)(2,1)S(1)}, u32[]{:S(2)}, u32[]{:S(2)}) collective-permute-start(bf16[1160,128]{1,0:T(8,128)(2,1)S(1)} %get-tuple-element.66), channel_id=1, source_target_pairs={{0,6},{2,4},{4,2},{6,0},{1,7},{3,5},{5,3},{7,1},{8,14},{10,12},{12... | collective-permute-start | bytes 890888 | tf_op jit(solution)/shard_map/ppermute | solution.py:204
  63.8 9.5 %collective-permute-done.22.refs_2_ = bf16[1160,128]{1,0:T(8,128)(2,1)S(1)} collective-permute-done((bf16[1160,128]{1,0:T(8,128)(2,1)S(1)}, bf16[1160,128]{1,0:T(8,128)(2,1)S(1)}, u32[]{:S(2)}, u32[]{:S(2)}) %collective-permute-start.22) | collective-permute-done | bytes 296992 | tf_op jit(solution)/shard_map/ppermute | solution.py:204
  73.3 3.7 %collective-permute-start.30 = (bf16[1160,128]{1,0:T(8,128)(2,1)S(1)}, bf16[1160,128]{1,0:T(8,128)(2,1)S(1)}, u32[]{:S(2)}, u32[]{:S(2)}) collective-permute-start(bf16[1160,128]{1,0:T(8,128)(2,1)S(1)} %get-tuple-element.74), channel_id=1, source_target_pairs={{0,6},{2,4},{4,2},{6,0},{1,7},{3,5},{5,3},{7,1},{8,14},{10,12},{12... | collective-permute-start | bytes 890888 | tf_op jit(solution)/shard_map/ppermute | solution.py:204
  77.1 3.2 %expert.5 = (bf16[72,2048]{1,0:T(8,128)(2,1)S(1)}, bf16[72,2048]{1,0:T(8,128)(2,1)S(1)}, bf16[72,2048]{1,0:T(8,128)(2,1)S(1)}, bf16[72,2048]{1,0:T(8,128)(2,1)S(1)}) custom-call(s32[3]{0:T(128)S(1)} %pad_add_fusion.1.expert_ref.scal_ref, s32[2]{0:T(128)S(1)} %bitcast.31, bf16[1160,128]{1,0:T(8,128)(2,1)S(1)} %get-tuple-element.55.refs_0_, ...), custom_call_target="tpu_custom_call" | custom-call | flops 1358954496 | bytes 4718592 | tf_op jit(solution)/shard_map/expert/pallas_call | solution.py:327
  80.3 1.8 %collective-permute-start.14 = (bf16[72,2048]{1,0:T(8,128)(2,1)S(1)}, bf16[72,2048]{1,0:T(8,128)(2,1)S(1)}, u32[]{:S(2)}, u32[]{:S(2)}) collective-permute-start(bf16[72,2048]{1,0:T(8,128)(2,1)S(1)} %get-tuple-element.60), channel_id=1, source_target_pairs={{0,2},{2,0},{4,6},{6,4},{1,3},{3,1},{5,7},{7,5},{8,10},{10,8},{12,... | collective-permute-start | bytes 884744 | tf_op jit(solution)/shard_map/ppermute | solution.py:204
  82.1 3.2 %expert.6 = (bf16[72,1024]{1,0:T(8,128)(2,1)S(1)}, bf16[72,1024]{1,0:T(8,128)(2,1)S(1)}, bf16[72,1024]{1,0:T(8,128)(2,1)S(1)}, bf16[72,1024]{1,0:T(8,128)(2,1)S(...) custom-call(s32[3]{0:T(128)S(1)} %pad_add_fusion.1.expert_ref.scal_r, ...), custom_call_target="tpu_custom_call" | custom-call | flops 1358954496 | bytes 4718592 | tf_op jit(solution)/shard_map/expert/pallas_call | solution.py:327
  87.2 2.4 %collective-permute-start.25 = (bf16[72,1024]{1,0:T(8,128)(2,1)S(1)}, bf16[72,1024]{1,0:T(8,128)(2,1)S(1)}, u32[]{:S(2)}, u32[]{:S(2)}) collective-permute-start(bf16[72,1024]{1,0:T(8,128)(2,1)S(1)} %get-tuple-element.69), channel_id=1, source_target_pairs={{0,4},{2,6},{4,0},{6,2},{1,5},{3,7},{5,1},{7,3},{8,12},{10,14},{12... | collective-permute-start | bytes 442376 | tf_op jit(solution)/shard_map/ppermute | solution.py:204
  89.6 2.9 %collective-permute-start.26 = (bf16[72,1024]{1,0:T(8,128)(2,1)S(1)}, bf16[72,1024]{1,0:T(8,128)(2,1)S(1)}, u32[]{:S(2)}, u32[]{:S(2)}) collective-permute-start(bf16[72,1024]{1,0:T(8,128)(2,1)S(1)} %get-tuple-element.70), channel_id=1, source_target_pairs={{0,6},{2,4},{4,2},{6,0},{1,7},{3,5},{5,3},{7,1},{8,14},{10,12},{12... | collective-permute-start | bytes 442376 | tf_op jit(solution)/shard_map/ppermute | solution.py:204
  92.5 3.2 %expert.7 = (bf16[72,1024]{1,0:T(8,128)(2,1)S(1)}, bf16[72,1024]{1,0:T(8,128)(2,1)S(1)}, bf16[72,1024]{1,0:T(8,128)(2,1)S(1)}, bf16[72,1024]{1,0:T(8,128)(2,1)S(...) custom-call(s32[3]{0:T(128)S(1)} %pad_add_fusion.1.expert_ref.scal_r, ...), custom_call_target="tpu_custom_call" | custom-call | flops 1358954496 | bytes 4718592 | tf_op jit(solution)/shard_map/expert/pallas_call | solution.py:327
  95.8 4.1 %collective-permute-done.24.refs_3_ = bf16[72,1024]{1,0:T(8,128)(2,1)S(1)} collective-permute-done((bf16[72,1024]{1,0:T(8,128)(2,1)S(1)}, bf16[72,1024]{1,0:T(8,128)(2,1)S(1)}, u32[]{:S(2)}, u32[]{:S(2)}) %collective-permute-start.24) | collective-permute-done | bytes 147488 | tf_op jit(solution)/shard_map/ppermute | solution.py:204
  99.9 2.5 %collective-permute-start.39 = (bf16[72,1024]{1,0:T(8,128)(2,1)S(1)}, bf16[72,1024]{1,0:T(8,128)(2,1)S(1)}, u32[]{:S(2)}, u32[]{:S(2)}) collective-permute-start(bf16[72,1024]{1,0:T(8,128)(2,1)S(1)} %get-tuple-element.84), channel_id=1, source_target_pairs={{0,2},{2,0},{4,6},{6,4},{1,3},{3,1},{5,7},{7,5},{8,10},{10,8},{12,... | collective-permute-start | bytes 442376 | tf_op jit(solution)/shard_map/ppermute | solution.py:204
  103.9 2.6 %collective-permute-start.41 = (bf16[72,1024]{1,0:T(8,128)(2,1)S(1)}, bf16[72,1024]{1,0:T(8,128)(2,1)S(1)}, u32[]{:S(2)}, u32[]{:S(2)}) collective-permute-start(bf16[72,1024]{1,0:T(8,128)(2,1)S(1)} %get-tuple-element.86), channel_id=1, source_target_pairs={{0,6},{2,4},{4,2},{6,0},{1,7},{3,5},{5,3},{7,1},{8,14},{10,12},{12... | collective-permute-start | bytes 442376 | tf_op jit(solution)/shard_map/ppermute | solution.py:204
  107.1 2.0 %collective-permute-start.31 = (bf16[72,1024]{1,0:T(8,128)(2,1)S(1)}, bf16[72,1024]{1,0:T(8,128)(2,1)S(1)}, u32[]{:S(2)}, u32[]{:S(2)}) collective-permute-start(bf16[72,1024]{1,0:T(8,128)(2,1)S(1)} %get-tuple-element.76), channel_id=1, source_target_pairs={{0,2},{2,0},{4,6},{6,4},{1,3},{3,1},{5,7},{7,5},{8,10},{10,8},{12,... | collective-permute-start | bytes 442376 | tf_op jit(solution)/shard_map/ppermute | solution.py:204
  109.0 8.4 %collective-permute-done.40.refs_4_ = bf16[72,1024]{1,0:T(8,128)(2,1)S(1)} collective-permute-done((bf16[72,1024]{1,0:T(8,128)(2,1)S(1)}, bf16[72,1024]{1,0:T(8,128)(2,1)S(1)}, u32[]{:S(2)}, u32[]{:S(2)}) %collective-permute-start.40) | collective-permute-done | bytes 147488 | tf_op jit(solution)/shard_map/ppermute | solution.py:204
  120.3 2.0 %collective-permute-start.36 = (bf16[72,1024]{1,0:T(8,128)(2,1)S(1)}, bf16[72,1024]{1,0:T(8,128)(2,1)S(1)}, u32[]{:S(2)}, u32[]{:S(2)}) collective-permute-start(bf16[72,1024]{1,0:T(8,128)(2,1)S(1)} %get-tuple-element.80), channel_id=1, source_target_pairs={{0,2},{2,0},{4,6},{6,4},{1,3},{3,1},{5,7},{7,5},{8,10},{10,8},{12,... | collective-permute-start | bytes 442376 | tf_op jit(solution)/shard_map/ppermute | solution.py:204
  122.9 5.3 %collective-permute-start.42 = (bf16[128,1024]{1,0:T(8,128)(2,1)S(1)}, bf16[128,1024]{1,0:T(8,128)(2,1)S(1)}, u32[]{:S(2)}, u32[]{:S(2)}) collective-permute-start(bf16[128,1024]{1,0:T(8,128)(2,1)S(1)} %shard_map.97), channel_id=1, source_target_pairs={{0,8},{8,0},{16,24},{24,16},{1,9},{9,1},{17,25},{25,17},{2,10},{10... | collective-permute-start | bytes 786440 | tf_op jit(solution)/shard_map/ppermute | solution.py:204
  128.3 3.4 %expert.4 = (bf16[72,2048]{1,0:T(8,128)(2,1)S(1)}, bf16[72,2048]{1,0:T(8,128)(2,1)S(1)}, bf16[72,2048]{1,0:T(8,128)(2,1)S(1)}, bf16[72,2048]{1,0:T(8,128)(2,1)S(1)}) custom-call(s32[3]{0:T(128)S(1)} %pad_add_fusion.1.expert_ref.scal_ref, s32[2]{0:T(128)S(1)} %bitcast.34, bf16[1160,128]{1,0:T(8,128)(2,1)S(1)} %get-tuple-element.47.refs_0_, ...), custom_call_target="tpu_custom_call" | custom-call | flops 1358954496 | bytes 4718592 | tf_op jit(solution)/shard_map/expert/pallas_call | solution.py:327
  131.6 2.0 %collective-permute-start.7 = (bf16[72,2048]{1,0:T(8,128)(2,1)S(1)}, bf16[72,2048]{1,0:T(8,128)(2,1)S(1)}, u32[]{:S(2)}, u32[]{:S(2)}) collective-permute-start(bf16[72,2048]{1,0:T(8,128)(2,1)S(1)} %get-tuple-element.52), channel_id=1, source_target_pairs={{0,2},{2,0},{4,6},{6,4},{1,3},{3,1},{5,7},{7,5},{8,10},{10,8},{12,... | collective-permute-start | bytes 884744 | tf_op jit(solution)/shard_map/ppermute | solution.py:204
  136.7 2.1 %collective-permute-start.17 = (bf16[128,2048]{1,0:T(8,128)(2,1)S(1)}, bf16[128,2048]{1,0:T(8,128)(2,1)S(1)}, u32[]{:S(2)}, u32[]{:S(2)}) collective-permute-start(bf16[128,2048]{1,0:T(8,128)(2,1)S(1)} %shard_map.92), channel_id=1, source_target_pairs={{0,8},{8,0},{16,24},{24,16},{1,9},{9,1},{17,25},{25,17},{2,10},{10... | collective-permute-start | bytes 1572872 | tf_op jit(solution)/shard_map/ppermute | solution.py:204
  138.9 5.9 %collective-permute-done.38.refs_5_ = bf16[72,1024]{1,0:T(8,128)(2,1)S(1)} collective-permute-done((bf16[72,1024]{1,0:T(8,128)(2,1)S(1)}, bf16[72,1024]{1,0:T(8,128)(2,1)S(1)}, u32[]{:S(2)}, u32[]{:S(2)}) %collective-permute-start.38) | collective-permute-done | bytes 147488 | tf_op jit(solution)/shard_map/ppermute | solution.py:204
  149.5 3.0 %collective-permute-start.35 = (bf16[128,1024]{1,0:T(8,128)(2,1)S(1)}, bf16[128,1024]{1,0:T(8,128)(2,1)S(1)}, u32[]{:S(2)}, u32[]{:S(2)}) collective-permute-start(bf16[128,1024]{1,0:T(8,128)(2,1)S(1)} %shard_map.96), channel_id=1, source_target_pairs={{0,16},{8,24},{16,0},{24,8},{1,17},{9,25},{17,1},{25,9},{2,18},{10... | collective-permute-start | bytes 786440 | tf_op jit(solution)/shard_map/ppermute | solution.py:204
  152.5 2.2 %collective-permute-done.8.refs_2_ = bf16[72,2048]{1,0:T(8,128)(2,1)S(1)} collective-permute-done((bf16[72,2048]{1,0:T(8,128)(2,1)S(1)}, bf16[72,2048]{1,0:T(8,128)(2,1)S(1)}, u32[]{:S(2)}, u32[]{:S(2)}) %collective-permute-start.8) | collective-permute-done | bytes 294944 | tf_op jit(solution)/shard_map/ppermute | solution.py:204
  154.7 6.5 %collective-permute-done.43.refs_6_ = bf16[128,1024]{1,0:T(8,128)(2,1)S(1)} collective-permute-done((bf16[128,1024]{1,0:T(8,128)(2,1)S(1)}, bf16[128,1024]{1,0:T(8,128)(2,1)S(1)}, u32[]{:S(2)}, u32[]{:S(2)}) %collective-permute-start.43) | collective-permute-done | bytes 262176 | tf_op jit(solution)/shard_map/ppermute | solution.py:204
  161.2 2.8 %collective-permute-done.35.refs_5_ = bf16[128,1024]{1,0:T(8,128)(2,1)S(1)} collective-permute-done((bf16[128,1024]{1,0:T(8,128)(2,1)S(1)}, bf16[128,1024]{1,0:T(8,128)(2,1)S(1)}, u32[]{:S(2)}, u32[]{:S(2)}) %collective-permute-start.35) | collective-permute-done | bytes 262176 | tf_op jit(solution)/shard_map/ppermute | solution.py:204
  164.0 2.5 %shard_map.99 = bf16[128,2048]{1,0:T(8,128)(2,1)} custom-call(s32[3]{0:T(128)S(1)} %pad_add_fusion.1.expert_ref.scal_ref, bf16[128,2176]{1,0:T(8,128)(2,1)S(1)} %get-tuple-element.46.ext_ref, bf16[72,2048]{1,0:T(8,128)(2,1)S(1)} %get-tuple-element.51.refs_0_, bf16[72,2048]{1,0:T(8,128)(2,1)S(1)} %collective-permute-done.7.refs_1_, ...), custom_call_target="tpu_custom_call" | custom-call | flops 150994944 | bytes 1810432 | tf_op jit(solution)/shard_map/pallas_call | solution.py:21
  (84 shorter events, 41.2 us)
Async XLA Ops:
  3.5 15.7 %collective-permute-start.10 = (bf16[128,2176]{1,0:T(8,128)(2,1)S(1)}, bf16[128,2176]{1,0:T(8,128)(2,1)S(1)}, u32[]{:S(2)}, u32[]{:S(2)}) collective-permute-start(bf16[128,2176]{1,0:T(8,128)(2,1)S(1)} %get-tuple-element.46.ext_ref), channel_id=1, source_target_pairs={{0,8},{8,0},{16,24},{24,16},{1,9},{9,1},{17,25},{25,17},{2,10},{10... | collective-permute-start | bytes 1671176 | tf_op jit(solution)/shard_map/ppermute | solution.py:204
  6.6 16.6 %collective-permute-start.19 = (bf16[128,2176]{1,0:T(8,128)(2,1)S(1)}, bf16[128,2176]{1,0:T(8,128)(2,1)S(1)}, u32[]{:S(2)}, u32[]{:S(2)}) collective-permute-start(bf16[128,2176]{1,0:T(8,128)(2,1)S(1)} %get-tuple-element.46.ext_ref), channel_id=1, source_target_pairs={{8,16},{16,8},{9,17},{17,9},{10,18},{18,10},{11,19},{19,11},{12,20... | collective-permute-start | bytes 1671176 | tf_op jit(solution)/shard_map/ppermute | solution.py:209
  7.3 69.7 %collective-permute-start.3 = (bf16[1024,768]{1,0:T(8,128)(2,1)}, bf16[1024,768]{1,0:T(8,128)(2,1)S(1)}, u32[]{:S(2)}, u32[]{:S(2)}) collective-permute-start(bf16[1024,768]{1,0:T(8,128)(2,1)} %bitcast.11), channel_id=1, source_target_pairs={{0,1},{1,0},{2,3},{3,2},{4,5},{5,4},{6,7},{7,6},{8,9},{9,8},{10,11... | collective-permute-start | bytes 4718600 | tf_op jit(solution)/shard_map/ppermute | solution.py:204
  19.3 13.3 %collective-permute-start.18 = (bf16[128,2176]{1,0:T(8,128)(2,1)S(1)}, bf16[128,2176]{1,0:T(8,128)(2,1)S(1)}, u32[]{:S(2)}, u32[]{:S(2)}) collective-permute-start(bf16[128,2176]{1,0:T(8,128)(2,1)S(1)} %collective-permute-done.10.refs_0_), channel_id=1, source_target_pairs={{8,16},{16,8},{9,17},{17,9},{10,18},{18,10},{11,19},{19,11},{12,20... | collective-permute-start | bytes 1671176 | tf_op jit(solution)/shard_map/ppermute | solution.py:209
  23.3 19.1 %collective-permute-start.20 = (bf16[128,2176]{1,0:T(8,128)(2,1)S(1)}, bf16[128,2176]{1,0:T(8,128)(2,1)S(1)}, u32[]{:S(2)}, u32[]{:S(2)}) collective-permute-start(bf16[128,2176]{1,0:T(8,128)(2,1)S(1)} %collective-permute-done.19.refs_0_), channel_id=1, source_target_pairs={{8,0},{16,24},{9,1},{17,25},{10,2},{18,26},{11,3},{19,27},{12,4},{... | collective-permute-start | bytes 1671176 | tf_op jit(solution)/shard_map/ppermute | solution.py:209
  24.6 20.8 %collective-permute-start.4 = (bf16[384,1024]{1,0:T(8,128)(2,1)}, bf16[384,1024]{1,0:T(8,128)(2,1)S(1)}, u32[]{:S(2)}, u32[]{:S(2)}) collective-permute-start(bf16[384,1024]{1,0:T(8,128)(2,1)} %bitcast.16), channel_id=1, source_target_pairs={{0,1},{1,0},{2,3},{3,2},{4,5},{5,4},{6,7},{7,6},{8,9},{9,8},{10,11... | collective-permute-start | bytes 2359304 | tf_op jit(solution)/shard_map/ppermute | solution.py:204
  32.6 25.8 %collective-permute-start.27 = (bf16[128,2176]{1,0:T(8,128)(2,1)S(1)}, bf16[128,2176]{1,0:T(8,128)(2,1)S(1)}, u32[]{:S(2)}, u32[]{:S(2)}) collective-permute-start(bf16[128,2176]{1,0:T(8,128)(2,1)S(1)} %collective-permute-done.18.refs_0_), channel_id=1, source_target_pairs={{8,0},{16,24},{9,1},{17,25},{10,2},{18,26},{11,3},{19,27},{12,4},{... | collective-permute-start | bytes 1671176 | tf_op jit(solution)/shard_map/ppermute | solution.py:209
  42.4 14.5 %collective-permute-start.12 = (bf16[1160,128]{1,0:T(8,128)(2,1)S(1)}, bf16[1160,128]{1,0:T(8,128)(2,1)S(1)}, u32[]{:S(2)}, u32[]{:S(2)}) collective-permute-start(bf16[1160,128]{1,0:T(8,128)(2,1)S(1)} %get-tuple-element.57), channel_id=1, source_target_pairs={{0,4},{2,6},{4,0},{6,2},{1,5},{3,7},{5,1},{7,3},{8,12},{10,14},{12... | collective-permute-start | bytes 890888 | tf_op jit(solution)/shard_map/ppermute | solution.py:204
  45.4 16.2 %collective-permute-start.13 = (bf16[1160,128]{1,0:T(8,128)(2,1)S(1)}, bf16[1160,128]{1,0:T(8,128)(2,1)S(1)}, u32[]{:S(2)}, u32[]{:S(2)}) collective-permute-start(bf16[1160,128]{1,0:T(8,128)(2,1)S(1)} %get-tuple-element.58), channel_id=1, source_target_pairs={{0,6},{2,4},{4,2},{6,0},{1,7},{3,5},{5,3},{7,1},{8,14},{10,12},{12... | collective-permute-start | bytes 890888 | tf_op jit(solution)/shard_map/ppermute | solution.py:204
  47.5 14.7 %collective-permute-start.21 = (bf16[1160,128]{1,0:T(8,128)(2,1)S(1)}, bf16[1160,128]{1,0:T(8,128)(2,1)S(1)}, u32[]{:S(2)}, u32[]{:S(2)}) collective-permute-start(bf16[1160,128]{1,0:T(8,128)(2,1)S(1)} %get-tuple-element.64), channel_id=1, source_target_pairs={{0,2},{2,0},{4,6},{6,4},{1,3},{3,1},{5,7},{7,5},{8,10},{10,8},{12,... | collective-permute-start | bytes 890888 | tf_op jit(solution)/shard_map/ppermute | solution.py:204
  56.9 16.4 %collective-permute-start.22 = (bf16[1160,128]{1,0:T(8,128)(2,1)S(1)}, bf16[1160,128]{1,0:T(8,128)(2,1)S(1)}, u32[]{:S(2)}, u32[]{:S(2)}) collective-permute-start(bf16[1160,128]{1,0:T(8,128)(2,1)S(1)} %get-tuple-element.65), channel_id=1, source_target_pairs={{0,4},{2,6},{4,0},{6,2},{1,5},{3,7},{5,1},{7,3},{8,12},{10,14},{12... | collective-permute-start | bytes 890888 | tf_op jit(solution)/shard_map/ppermute | solution.py:204
  58.4 21.9 %collective-permute-start.23 = (bf16[1160,128]{1,0:T(8,128)(2,1)S(1)}, bf16[1160,128]{1,0:T(8,128)(2,1)S(1)}, u32[]{:S(2)}, u32[]{:S(2)}) collective-permute-start(bf16[1160,128]{1,0:T(8,128)(2,1)S(1)} %get-tuple-element.66), channel_id=1, source_target_pairs={{0,6},{2,4},{4,2},{6,0},{1,7},{3,5},{5,3},{7,1},{8,14},{10,12},{12... | collective-permute-start | bytes 890888 | tf_op jit(solution)/shard_map/ppermute | solution.py:204
  61.6 23.7 %collective-permute-start.28 = (bf16[1160,128]{1,0:T(8,128)(2,1)S(1)}, bf16[1160,128]{1,0:T(8,128)(2,1)S(1)}, u32[]{:S(2)}, u32[]{:S(2)}) collective-permute-start(bf16[1160,128]{1,0:T(8,128)(2,1)S(1)} %get-tuple-element.72), channel_id=1, source_target_pairs={{0,2},{2,0},{4,6},{6,4},{1,3},{3,1},{5,7},{7,5},{8,10},{10,8},{12,... | collective-permute-start | bytes 890888 | tf_op jit(solution)/shard_map/ppermute | solution.py:204
  62.2 25.0 %collective-permute-start.29 = (bf16[1160,128]{1,0:T(8,128)(2,1)S(1)}, bf16[1160,128]{1,0:T(8,128)(2,1)S(1)}, u32[]{:S(2)}, u32[]{:S(2)}) collective-permute-start(bf16[1160,128]{1,0:T(8,128)(2,1)S(1)} %get-tuple-element.73), channel_id=1, source_target_pairs={{0,4},{2,6},{4,0},{6,2},{1,5},{3,7},{5,1},{7,3},{8,12},{10,14},{12... | collective-permute-start | bytes 890888 | tf_op jit(solution)/shard_map/ppermute | solution.py:204
  73.3 16.3 %collective-permute-start.30 = (bf16[1160,128]{1,0:T(8,128)(2,1)S(1)}, bf16[1160,128]{1,0:T(8,128)(2,1)S(1)}, u32[]{:S(2)}, u32[]{:S(2)}) collective-permute-start(bf16[1160,128]{1,0:T(8,128)(2,1)S(1)} %get-tuple-element.74), channel_id=1, source_target_pairs={{0,6},{2,4},{4,2},{6,0},{1,7},{3,5},{5,3},{7,1},{8,14},{10,12},{12... | collective-permute-start | bytes 890888 | tf_op jit(solution)/shard_map/ppermute | solution.py:204
  77.1 18.7 %collective-permute-start.2 = (bf16[1160,128]{1,0:T(8,128)(2,1)S(1)}, bf16[1160,128]{1,0:T(8,128)(2,1)S(1)}, u32[]{:S(2)}, u32[]{:S(2)}) collective-permute-start(bf16[1160,128]{1,0:T(8,128)(2,1)S(1)} %get-tuple-element.50), channel_id=1, source_target_pairs={{0,6},{2,4},{4,2},{6,0},{1,7},{3,5},{5,3},{7,1},{8,14},{10,12},{12... | collective-permute-start | bytes 890888 | tf_op jit(solution)/shard_map/ppermute | solution.py:204
  80.3 26.2 %collective-permute-start.14 = (bf16[72,2048]{1,0:T(8,128)(2,1)S(1)}, bf16[72,2048]{1,0:T(8,128)(2,1)S(1)}, u32[]{:S(2)}, u32[]{:S(2)}) collective-permute-start(bf16[72,2048]{1,0:T(8,128)(2,1)S(1)} %get-tuple-element.60), channel_id=1, source_target_pairs={{0,2},{2,0},{4,6},{6,4},{1,3},{3,1},{5,7},{7,5},{8,10},{10,8},{12,... | collective-permute-start | bytes 884744 | tf_op jit(solution)/shard_map/ppermute | solution.py:204
  85.3 14.6 %collective-permute-start.24 = (bf16[72,1024]{1,0:T(8,128)(2,1)S(1)}, bf16[72,1024]{1,0:T(8,128)(2,1)S(1)}, u32[]{:S(2)}, u32[]{:S(2)}) collective-permute-start(bf16[72,1024]{1,0:T(8,128)(2,1)S(1)} %get-tuple-element.68), channel_id=1, source_target_pairs={{0,2},{2,0},{4,6},{6,4},{1,3},{3,1},{5,7},{7,5},{8,10},{10,8},{12,... | collective-permute-start | bytes 442376 | tf_op jit(solution)/shard_map/ppermute | solution.py:204
  87.2 15.1 %collective-permute-start.25 = (bf16[72,1024]{1,0:T(8,128)(2,1)S(1)}, bf16[72,1024]{1,0:T(8,128)(2,1)S(1)}, u32[]{:S(2)}, u32[]{:S(2)}) collective-permute-start(bf16[72,1024]{1,0:T(8,128)(2,1)S(1)} %get-tuple-element.69), channel_id=1, source_target_pairs={{0,4},{2,6},{4,0},{6,2},{1,5},{3,7},{5,1},{7,3},{8,12},{10,14},{12... | collective-permute-start | bytes 442376 | tf_op jit(solution)/shard_map/ppermute | solution.py:204
  89.6 14.3 %collective-permute-start.26 = (bf16[72,1024]{1,0:T(8,128)(2,1)S(1)}, bf16[72,1024]{1,0:T(8,128)(2,1)S(1)}, u32[]{:S(2)}, u32[]{:S(2)}) collective-permute-start(bf16[72,1024]{1,0:T(8,128)(2,1)S(1)} %get-tuple-element.70), channel_id=1, source_target_pairs={{0,6},{2,4},{4,2},{6,0},{1,7},{3,5},{5,3},{7,1},{8,14},{10,12},{12... | collective-permute-start | bytes 442376 | tf_op jit(solution)/shard_map/ppermute | solution.py:204
  95.7 24.6 %collective-permute-start.15 = (bf16[72,2048]{1,0:T(8,128)(2,1)S(1)}, bf16[72,2048]{1,0:T(8,128)(2,1)S(1)}, u32[]{:S(2)}, u32[]{:S(2)}) collective-permute-start(bf16[72,2048]{1,0:T(8,128)(2,1)S(1)} %get-tuple-element.61), channel_id=1, source_target_pairs={{0,4},{2,6},{4,0},{6,2},{1,5},{3,7},{5,1},{7,3},{8,12},{10,14},{12... | collective-permute-start | bytes 884744 | tf_op jit(solution)/shard_map/ppermute | solution.py:204
  102.4 15.1 %collective-permute-start.40 = (bf16[72,1024]{1,0:T(8,128)(2,1)S(1)}, bf16[72,1024]{1,0:T(8,128)(2,1)S(1)}, u32[]{:S(2)}, u32[]{:S(2)}) collective-permute-start(bf16[72,1024]{1,0:T(8,128)(2,1)S(1)} %get-tuple-element.85), channel_id=1, source_target_pairs={{0,4},{2,6},{4,0},{6,2},{1,5},{3,7},{5,1},{7,3},{8,12},{10,14},{12... | collective-permute-start | bytes 442376 | tf_op jit(solution)/shard_map/ppermute | solution.py:204
  103.9 14.1 %collective-permute-start.41 = (bf16[72,1024]{1,0:T(8,128)(2,1)S(1)}, bf16[72,1024]{1,0:T(8,128)(2,1)S(1)}, u32[]{:S(2)}, u32[]{:S(2)}) collective-permute-start(bf16[72,1024]{1,0:T(8,128)(2,1)S(1)} %get-tuple-element.86), channel_id=1, source_target_pairs={{0,6},{2,4},{4,2},{6,0},{1,7},{3,5},{5,3},{7,1},{8,14},{10,12},{12... | collective-permute-start | bytes 442376 | tf_op jit(solution)/shard_map/ppermute | solution.py:204
  106.5 28.5 %collective-permute-start.16 = (bf16[72,2048]{1,0:T(8,128)(2,1)S(1)}, bf16[72,2048]{1,0:T(8,128)(2,1)S(1)}, u32[]{:S(2)}, u32[]{:S(2)}) collective-permute-start(bf16[72,2048]{1,0:T(8,128)(2,1)S(1)} %get-tuple-element.62), channel_id=1, source_target_pairs={{0,6},{2,4},{4,2},{6,0},{1,7},{3,5},{5,3},{7,1},{8,14},{10,12},{12... | collective-permute-start | bytes 884744 | tf_op jit(solution)/shard_map/ppermute | solution.py:204
  107.1 15.3 %collective-permute-start.31 = (bf16[72,1024]{1,0:T(8,128)(2,1)S(1)}, bf16[72,1024]{1,0:T(8,128)(2,1)S(1)}, u32[]{:S(2)}, u32[]{:S(2)}) collective-permute-start(bf16[72,1024]{1,0:T(8,128)(2,1)S(1)} %get-tuple-element.76), channel_id=1, source_target_pairs={{0,2},{2,0},{4,6},{6,4},{1,3},{3,1},{5,7},{7,5},{8,10},{10,8},{12,... | collective-permute-start | bytes 442376 | tf_op jit(solution)/shard_map/ppermute | solution.py:204
  118.0 13.6 %collective-permute-start.33 = (bf16[72,1024]{1,0:T(8,128)(2,1)S(1)}, bf16[72,1024]{1,0:T(8,128)(2,1)S(1)}, u32[]{:S(2)}, u32[]{:S(2)}) collective-permute-start(bf16[72,1024]{1,0:T(8,128)(2,1)S(1)} %get-tuple-element.78), channel_id=1, source_target_pairs={{0,6},{2,4},{4,2},{6,0},{1,7},{3,5},{5,3},{7,1},{8,14},{10,12},{12... | collective-permute-start | bytes 442376 | tf_op jit(solution)/shard_map/ppermute | solution.py:204
  120.3 16.4 %collective-permute-start.36 = (bf16[72,1024]{1,0:T(8,128)(2,1)S(1)}, bf16[72,1024]{1,0:T(8,128)(2,1)S(1)}, u32[]{:S(2)}, u32[]{:S(2)}) collective-permute-start(bf16[72,1024]{1,0:T(8,128)(2,1)S(1)} %get-tuple-element.80), channel_id=1, source_target_pairs={{0,2},{2,0},{4,6},{6,4},{1,3},{3,1},{5,7},{7,5},{8,10},{10,8},{12,... | collective-permute-start | bytes 442376 | tf_op jit(solution)/shard_map/ppermute | solution.py:204
  122.3 16.4 %collective-permute-start.37 = (bf16[72,1024]{1,0:T(8,128)(2,1)S(1)}, bf16[72,1024]{1,0:T(8,128)(2,1)S(1)}, u32[]{:S(2)}, u32[]{:S(2)}) collective-permute-start(bf16[72,1024]{1,0:T(8,128)(2,1)S(1)} %get-tuple-element.81), channel_id=1, source_target_pairs={{0,4},{2,6},{4,0},{6,2},{1,5},{3,7},{5,1},{7,3},{8,12},{10,14},{12... | collective-permute-start | bytes 442376 | tf_op jit(solution)/shard_map/ppermute | solution.py:204
  122.9 22.5 %collective-permute-start.42 = (bf16[128,1024]{1,0:T(8,128)(2,1)S(1)}, bf16[128,1024]{1,0:T(8,128)(2,1)S(1)}, u32[]{:S(2)}, u32[]{:S(2)}) collective-permute-start(bf16[128,1024]{1,0:T(8,128)(2,1)S(1)} %shard_map.97), channel_id=1, source_target_pairs={{0,8},{8,0},{16,24},{24,16},{1,9},{9,1},{17,25},{25,17},{2,10},{10... | collective-permute-start | bytes 786440 | tf_op jit(solution)/shard_map/ppermute | solution.py:204
  131.6 17.8 %collective-permute-start.7 = (bf16[72,2048]{1,0:T(8,128)(2,1)S(1)}, bf16[72,2048]{1,0:T(8,128)(2,1)S(1)}, u32[]{:S(2)}, u32[]{:S(2)}) collective-permute-start(bf16[72,2048]{1,0:T(8,128)(2,1)S(1)} %get-tuple-element.52), channel_id=1, source_target_pairs={{0,2},{2,0},{4,6},{6,4},{1,3},{3,1},{5,7},{7,5},{8,10},{10,8},{12,... | collective-permute-start | bytes 884744 | tf_op jit(solution)/shard_map/ppermute | solution.py:204
  136.7 18.0 %collective-permute-start.17 = (bf16[128,2048]{1,0:T(8,128)(2,1)S(1)}, bf16[128,2048]{1,0:T(8,128)(2,1)S(1)}, u32[]{:S(2)}, u32[]{:S(2)}) collective-permute-start(bf16[128,2048]{1,0:T(8,128)(2,1)S(1)} %shard_map.92), channel_id=1, source_target_pairs={{0,8},{8,0},{16,24},{24,16},{1,9},{9,1},{17,25},{25,17},{2,10},{10... | collective-permute-start | bytes 1572872 | tf_op jit(solution)/shard_map/ppermute | solution.py:204
  149.5 14.5 %collective-permute-start.35 = (bf16[128,1024]{1,0:T(8,128)(2,1)S(1)}, bf16[128,1024]{1,0:T(8,128)(2,1)S(1)}, u32[]{:S(2)}, u32[]{:S(2)}) collective-permute-start(bf16[128,1024]{1,0:T(8,128)(2,1)S(1)} %shard_map.96), channel_id=1, source_target_pairs={{0,16},{8,24},{16,0},{24,8},{1,17},{9,25},{17,1},{25,9},{2,18},{10... | collective-permute-start | bytes 786440 | tf_op jit(solution)/shard_map/ppermute | solution.py:204
  (18 other events, 473.5 us)

commit v3 on v2

--- a/solution.py
+++ b/solution.py
@@ -76,7 +76,7 @@
         outs[q][width // LANES * rows :] = jnp.dot(tenant, picked, preferred_element_type=F32).astype(BF16)
 
 
-def first_body(top, rows, expert_ref, tok_any, meta_ref, ext_ref, *refs):
+def first_body(top, rows, expert_ref, tok_any, meta_ref, ext_ref, plan_ref, *refs):
     outs, sem = refs[:INNER], refs[INNER]
     tok, width = tok_any.shape
     copy = pltpu.make_async_copy(tok_any, ext_ref.at[:, pl.ds(0, width)], sem)
@@ -105,12 +105,15 @@
     slots = packing(meta, expert_ref[0], top)
     copy.wait()
     pack_rows(slots, ext_ref[...], meta_t, outs, top, rows)
+    plan_ref[...] = plan_of(slots, meta, expert_ref[0], top)
 
 
 def pack_body(top, rows, width, scal_ref, *refs):
-    wide = either(scal_ref, refs[:-INNER])
+    wide = either(scal_ref, refs[: -INNER - 1])
     meta = wide[:, width:].astype(F32)
-    pack_rows(packing(meta, scal_ref[0], top), wide, meta.T, refs[-INNER:], top, rows)
+    slots = packing(meta, scal_ref[0], top)
+    pack_rows(slots, wide, meta.T, refs[-INNER:], top, rows)
+    refs[-INNER - 1][...] = plan_of(slots, meta, scal_ref[0], top)
 
 
 def expert_body(rows, stores, parts, scal_ref, adapted_ref, *refs):
@@ -166,34 +169,39 @@
             outs[q * parts + i][...] = y_ref[q * rows : (q + 1) * rows, i * each : (i + 1) * each]
 
 
-def weighted(expert, meta, ys, top, rows):
-    slots = packing(meta, expert, top)
+def plan_of(slots, meta, expert, top):
     lane = iota(meta.shape, 1)
     chosen = jnp.where(lane < top, meta, -1.0)
     share = sum(pltpu.roll(meta, LANES - 32 * (i + 1), 1) for i in range(3))
-    total = None
+    plan = jnp.zeros(meta.shape, F32)
     for q in range(INNER):
         target = lax.bitwise_xor(expert, q).astype(F32)
         mine = jnp.sum(jnp.where(chosen == target, share, 0.0), axis=1, keepdims=True)
-        spot = iota((meta.shape[0], rows), 1).astype(F32)
-        spread = jnp.where(spot == slots[q], 1.0, 0.0).astype(BF16)
-        part = jnp.dot(spread, ys[q][...], preferred_element_type=F32) * mine
+        plan = jnp.where(lane == q, slots[q], plan)
+        plan = jnp.where(lane == INNER + q, mine, plan)
+    return plan
+
+
+def weighted(plan, ys, rows):
+    spot = iota((plan.shape[0], rows), 1).astype(F32)
+    total = None
+    for q in range(INNER):
+        spread = jnp.where(spot == plan[:, q : q + 1], 1.0, 0.0).astype(BF16)
+        part = jnp.dot(spread, ys[q][...], preferred_element_type=F32) * plan[:, INNER + q : INNER + q + 1]
         total = part if total is None else total + part
     return total
 
 
-def partial_body(top, rows, width, held, scal_ref, *refs):
-    meta = either(scal_ref, refs[:held], slice(width, None)).astype(F32)
-    refs = refs[held:]
-    total = weighted(scal_ref[0], meta, refs[:INNER], top, rows)
+def sum_body(rows, plan_ref, *refs):
+    total = weighted(plan_ref[...], refs[:INNER], rows)
     for other in refs[INNER:-1]:
         total = total + other[...].astype(F32)
-    refs[-1][...] = total.astype(BF16)
-
-
-def final_body(top, rows, width, splits, scal_ref, ext_ref, *refs):
-    total = weighted(scal_ref[0], ext_ref[:, width:].astype(F32), refs[:INNER], top, rows)
-    others, out = list(refs[INNER:-1]), refs[-1]
+    refs[-1][...] = total.astype(refs[-1].dtype)
+
+
+def final_body(splits, total_ref, *refs):
+    total = total_ref[...]
+    others, out = list(refs[:-1]), refs[-1]
     for count in splits:
         pieces = [others.pop(0)[...].astype(F32) for _ in range(count)]
         total = total + (pieces[0] if count == 1 else jnp.concatenate(pieces, axis=1))
@@ -256,6 +264,7 @@
     ends = jnp.logical_or(place == 0, place == outer - 1)
     scal = jnp.stack([expert, store, ends.astype(jnp.int32)]).astype(jnp.int32)
     packed = jax.ShapeDtypeStruct((width // LANES * rows + 8, LANES), BF16)
+    plan_shape = jax.ShapeDtypeStruct((tok, LANES), F32)
     ext_shape = jax.ShapeDtypeStruct((tok, wide), BF16)
     sums = jax.ShapeDtypeStruct((tok, width), BF16)
 
@@ -266,9 +275,9 @@
     meta = ints.astype(F32) + jnp.pad(router_weight_logits.T, ((top + 8, 0), (0, 0)))
     first = pl.pallas_call(
         functools.partial(first_body, top, rows),
-        out_shape=[ext_shape] + [packed] * INNER,
+        out_shape=[ext_shape, plan_shape] + [packed] * INNER,
         in_specs=[SMEM, pl.BlockSpec(memory_space=pl.ANY), VMEM],
-        out_specs=[VMEM] * (1 + INNER),
+        out_specs=[VMEM] * (2 + INNER),
         scratch_shapes=[pltpu.SemaphoreType.DMA],
         compiler_params=pltpu.CompilerParams(vmem_limit_bytes=20 * 1024 * 1024),
         cost_estimate=pl.CostEstimate(flops=move_flops, bytes_accessed=move_bytes, transcendentals=0),
@@ -280,7 +289,7 @@
         blocks = [(first[0],)]
         for d in range(1, outer):
             blocks.append((swap(blocks[d - lowest(d)][0], "outer", lowest(d)),))
-    rows_of = [first[1:]]
+    plans, rows_of = [first[1]], [first[2:]]
 
     ups = [gate_up_weight[0]]
     downs = [down_weight[0]]
@@ -293,15 +302,15 @@
         fup.append(swap(fup[0], "store", r))
 
     for d in range(1, outer):
-        rows_of.append(
-            call(
-                functools.partial(pack_body, top, rows, width),
-                [packed] * INNER,
-                [[scal], *blocks[d]],
-                move_flops,
-                move_bytes,
-            )
+        got = call(
+            functools.partial(pack_body, top, rows, width),
+            [plan_shape] + [packed] * INNER,
+            [[scal], *blocks[d]],
+            move_flops,
+            move_bytes,
         )
+        plans.append(got[0])
+        rows_of.append(got[1:])
     arrived = [[r[0]] + [swap(r[q], "inner", q) for q in range(1, INNER)] for r in rows_of]
 
     backs = []
@@ -336,9 +345,9 @@
         for i, rows_back in enumerate(backs[d]):
             sums.append(
                 call(
-                    functools.partial(partial_body, top, rows, width, len(blocks[d])),
+                    functools.partial(sum_body, rows),
                     jax.ShapeDtypeStruct((tok, width // len(backs[d])), BF16),
-                    [[scal], *blocks[d], *rows_back, *(m[i] for m in more)],
+                    [[], plans[d], *rows_back, *(m[i] for m in more)],
                     move_flops,
                     move_bytes,
                 )
@@ -346,12 +355,19 @@
         return sums
 
     others = joining(0, [1 << bit for bit in range(outer.bit_length()) if 1 << bit < outer])
-    return call(
-        functools.partial(final_body, top, rows, width, [len(other) for other in others]),
-        sums,
-        [[scal], first[0]] + backs[0][0] + sum(others, []),
+    own = call(
+        functools.partial(sum_body, rows),
+        jax.ShapeDtypeStruct((tok, width), F32),
+        [[], plans[0], *backs[0][0]],
         move_flops,
         move_bytes,
+    )
+    return call(
+        functools.partial(final_body, [len(other) for other in others]),
+        sums,
+        [[], own] + sum(others, []),
+        tok * width,
+        8 * tok * width,
     )
 
 

time: 167 us -> 164 us (0.982)
  Pallas kernels: 28.3 us -> 23.5 us
  waiting for transfers between devices: 75.2 us -> 77.2 us
    pallas_call x9 -> x10, Pallas kernels: 13.8 us -> 8.93 us  [call(): pl.pallas_call(body, out_shape=outs, in_specs=[SMEM] * len(smem) + [VMEM]...]
    ppermute x40, waiting for transfers between devices: 73.8 us -> 75.8 us  [swap(): lax.ppermute(array, axis, [(i, i ^ distance) for i in range(lax.axis_size...]
  transfers between devices with their start and end apart: 44 -> 44, of which waited for: 17 -> 18; matrix products, arithmetic and copies ran while one was open for 0% -> 0% of each run, Pallas kernels for 15% -> 13%
where the time goes in v3:
time: 164 us
  waiting for transfers between devices  77.2 us (47%)
  starting transfers between devices  60.7 us (37%)
  Pallas kernels  23.5 us (14%)
    ppermute x40, waiting for transfers between devices, swap(): lax.ppermute(array, axis, [(i, i ^ distance) for i in range(lax.axis_size...  75.8 us
    ppermute x40, starting transfers between devices, swap(): lax.ppermute(array, axis, [(i, i ^ distance) for i in range(lax.axis_size...  56.8 us
    pallas_call x4, Pallas kernels, shards(): got = kernel(scal, adapted[:, 0], *arrived[d], *ups, *downs, *fin, *fup)  12.9 us
    pallas_call x10, Pallas kernels, call(): pl.pallas_call(body, out_shape=outs, in_specs=[SMEM] * len(smem) + [VMEM]...  8.93 us
    ppermute x4, starting transfers between devices, send(): return lax.ppermute(array, 'outer', pairs)  3.93 us
  transfers between devices with their start and end apart: 44, of which 18 were waited for; matrix products, arithmetic and copies ran while one was open for 0% of the time, Pallas kernels for 13%

profile of v3, /device:TPU:0, one launch (start us, length us, event | category | flops | bytes accessed | tf_op | source)
XLA Modules:
  0.0 163.6 jit_solution(13803591263539504524)
XLA Ops:
  3.5 3.1 %collective-permute-start.10 = (bf16[128,2176]{1,0:T(8,128)(2,1)S(1)}, bf16[128,2176]{1,0:T(8,128)(2,1)S(1)}, u32[]{:S(2)}, u32[]{:S(2)}) collective-permute-start(bf16[128,2176]{1,0:T(8,128)(2,1)S(1)} %get-tuple-element.59), channel_id=1, source_target_pairs={{0,8},{8,0},{16,24},{24,16},{1,9},{9,1},{17,25},{25,17},{2,10},{10... | collective-permute-start | bytes 1671176 | tf_op jit(solution)/shard_map/ppermute | solution.py:212
  7.4 11.9 %collective-permute-done.10.refs_0_ = bf16[128,2176]{1,0:T(8,128)(2,1)S(1)} collective-permute-done((bf16[128,2176]{1,0:T(8,128)(2,1)S(1)}, bf16[128,2176]{1,0:T(8,128)(2,1)S(1)}, u32[]{:S(2)}, u32[]{:S(2)}) %collective-permute-start.10) | collective-permute-done | bytes 557088 | tf_op jit(solution)/shard_map/ppermute | solution.py:212
  24.7 6.2 %collective-permute-done.refs_1_ = bf16[1160,128]{1,0:T(8,128)(2,1)S(1)} collective-permute-done((bf16[1160,128]{1,0:T(8,128)(2,1)S(1)}, bf16[1160,128]{1,0:T(8,128)(2,1)S(1)}, u32[]{:S(2)}, u32[]{:S(2)}) %collective-permute-start) | collective-permute-done | bytes 296992 | tf_op jit(solution)/shard_map/ppermute | solution.py:212
  35.4 4.0 %collective-permute-done.1.refs_2_ = bf16[1160,128]{1,0:T(8,128)(2,1)S(1)} collective-permute-done((bf16[1160,128]{1,0:T(8,128)(2,1)S(1)}, bf16[1160,128]{1,0:T(8,128)(2,1)S(1)}, u32[]{:S(2)}, u32[]{:S(2)}) %collective-permute-start.1) | collective-permute-done | bytes 296992 | tf_op jit(solution)/shard_map/ppermute | solution.py:212
  47.5 2.5 %collective-permute-start.21 = (bf16[1160,128]{1,0:T(8,128)(2,1)S(1)}, bf16[1160,128]{1,0:T(8,128)(2,1)S(1)}, u32[]{:S(2)}, u32[]{:S(2)}) collective-permute-start(bf16[1160,128]{1,0:T(8,128)(2,1)S(1)} %get-tuple-element.71), channel_id=1, source_target_pairs={{0,2},{2,0},{4,6},{6,4},{1,3},{3,1},{5,7},{7,5},{8,10},{10,8},{12,... | collective-permute-start | bytes 890888 | tf_op jit(solution)/shard_map/ppermute | solution.py:212
  50.0 6.9 %collective-permute-done.12.refs_2_ = bf16[1160,128]{1,0:T(8,128)(2,1)S(1)} collective-permute-done((bf16[1160,128]{1,0:T(8,128)(2,1)S(1)}, bf16[1160,128]{1,0:T(8,128)(2,1)S(1)}, u32[]{:S(2)}, u32[]{:S(2)}) %collective-permute-start.12) | collective-permute-done | bytes 296992 | tf_op jit(solution)/shard_map/ppermute | solution.py:212
  58.4 1.7 %collective-permute-start.23 = (bf16[1160,128]{1,0:T(8,128)(2,1)S(1)}, bf16[1160,128]{1,0:T(8,128)(2,1)S(1)}, u32[]{:S(2)}, u32[]{:S(2)}) collective-permute-start(bf16[1160,128]{1,0:T(8,128)(2,1)S(1)} %get-tuple-element.73), channel_id=1, source_target_pairs={{0,6},{2,4},{4,2},{6,0},{1,7},{3,5},{5,3},{7,1},{8,14},{10,12},{12... | collective-permute-start | bytes 890888 | tf_op jit(solution)/shard_map/ppermute | solution.py:212
  63.8 9.5 %collective-permute-done.22.refs_2_ = bf16[1160,128]{1,0:T(8,128)(2,1)S(1)} collective-permute-done((bf16[1160,128]{1,0:T(8,128)(2,1)S(1)}, bf16[1160,128]{1,0:T(8,128)(2,1)S(1)}, u32[]{:S(2)}, u32[]{:S(2)}) %collective-permute-start.22) | collective-permute-done | bytes 296992 | tf_op jit(solution)/shard_map/ppermute | solution.py:212
  73.4 3.8 %collective-permute-start.30 = (bf16[1160,128]{1,0:T(8,128)(2,1)S(1)}, bf16[1160,128]{1,0:T(8,128)(2,1)S(1)}, u32[]{:S(2)}, u32[]{:S(2)}) collective-permute-start(bf16[1160,128]{1,0:T(8,128)(2,1)S(1)} %get-tuple-element.82), channel_id=1, source_target_pairs={{0,6},{2,4},{4,2},{6,0},{1,7},{3,5},{5,3},{7,1},{8,14},{10,12},{12... | collective-permute-start | bytes 890888 | tf_op jit(solution)/shard_map/ppermute | solution.py:212
  77.2 3.2 %expert.5 = (bf16[72,2048]{1,0:T(8,128)(2,1)S(1)}, bf16[72,2048]{1,0:T(8,128)(2,1)S(1)}, bf16[72,2048]{1,0:T(8,128)(2,1)S(1)}, bf16[72,2048]{1,0:T(8,128)(2,1)S(1)}) custom-call(s32[3]{0:T(128)S(1)} %pad_add_fusion.1.expert_ref.scal_ref, s32[2]{0:T(128)S(1)} %bitcast.31, bf16[1160,128]{1,0:T(8,128)(2,1)S(1)} %get-tuple-element.61.refs_0_, ...), custom_call_target="tpu_custom_call" | custom-call | flops 1358954496 | bytes 4718592 | tf_op jit(solution)/shard_map/expert/pallas_call | solution.py:336
  80.4 1.8 %collective-permute-start.14 = (bf16[72,2048]{1,0:T(8,128)(2,1)S(1)}, bf16[72,2048]{1,0:T(8,128)(2,1)S(1)}, u32[]{:S(2)}, u32[]{:S(2)}) collective-permute-start(bf16[72,2048]{1,0:T(8,128)(2,1)S(1)} %get-tuple-element.66), channel_id=1, source_target_pairs={{0,2},{2,0},{4,6},{6,4},{1,3},{3,1},{5,7},{7,5},{8,10},{10,8},{12,... | collective-permute-start | bytes 884744 | tf_op jit(solution)/shard_map/ppermute | solution.py:212
  82.2 3.2 %expert.6 = (bf16[72,1024]{1,0:T(8,128)(2,1)S(1)}, bf16[72,1024]{1,0:T(8,128)(2,1)S(1)}, bf16[72,1024]{1,0:T(8,128)(2,1)S(1)}, bf16[72,1024]{1,0:T(8,128)(2,1)S(...) custom-call(s32[3]{0:T(128)S(1)} %pad_add_fusion.1.expert_ref.scal_r, ...), custom_call_target="tpu_custom_call" | custom-call | flops 1358954496 | bytes 4718592 | tf_op jit(solution)/shard_map/expert/pallas_call | solution.py:336
  87.2 2.4 %collective-permute-start.25 = (bf16[72,1024]{1,0:T(8,128)(2,1)S(1)}, bf16[72,1024]{1,0:T(8,128)(2,1)S(1)}, u32[]{:S(2)}, u32[]{:S(2)}) collective-permute-start(bf16[72,1024]{1,0:T(8,128)(2,1)S(1)} %get-tuple-element.76), channel_id=1, source_target_pairs={{0,4},{2,6},{4,0},{6,2},{1,5},{3,7},{5,1},{7,3},{8,12},{10,14},{12... | collective-permute-start | bytes 442376 | tf_op jit(solution)/shard_map/ppermute | solution.py:212
  89.6 2.9 %collective-permute-start.26 = (bf16[72,1024]{1,0:T(8,128)(2,1)S(1)}, bf16[72,1024]{1,0:T(8,128)(2,1)S(1)}, u32[]{:S(2)}, u32[]{:S(2)}) collective-permute-start(bf16[72,1024]{1,0:T(8,128)(2,1)S(1)} %get-tuple-element.77), channel_id=1, source_target_pairs={{0,6},{2,4},{4,2},{6,0},{1,7},{3,5},{5,3},{7,1},{8,14},{10,12},{12... | collective-permute-start | bytes 442376 | tf_op jit(solution)/shard_map/ppermute | solution.py:212
  92.6 3.2 %expert.7 = (bf16[72,1024]{1,0:T(8,128)(2,1)S(1)}, bf16[72,1024]{1,0:T(8,128)(2,1)S(1)}, bf16[72,1024]{1,0:T(8,128)(2,1)S(1)}, bf16[72,1024]{1,0:T(8,128)(2,1)S(...) custom-call(s32[3]{0:T(128)S(1)} %pad_add_fusion.1.expert_ref.scal_r, ...), custom_call_target="tpu_custom_call" | custom-call | flops 1358954496 | bytes 4718592 | tf_op jit(solution)/shard_map/expert/pallas_call | solution.py:336
  95.8 4.1 %collective-permute-done.24.refs_1_ = bf16[72,1024]{1,0:T(8,128)(2,1)S(1)} collective-permute-done((bf16[72,1024]{1,0:T(8,128)(2,1)S(1)}, bf16[72,1024]{1,0:T(8,128)(2,1)S(1)}, u32[]{:S(2)}, u32[]{:S(2)}) %collective-permute-start.24) | collective-permute-done | bytes 147488 | tf_op jit(solution)/shard_map/ppermute | solution.py:212
  99.9 2.5 %collective-permute-start.39 = (bf16[72,1024]{1,0:T(8,128)(2,1)S(1)}, bf16[72,1024]{1,0:T(8,128)(2,1)S(1)}, u32[]{:S(2)}, u32[]{:S(2)}) collective-permute-start(bf16[72,1024]{1,0:T(8,128)(2,1)S(1)} %get-tuple-element.92), channel_id=1, source_target_pairs={{0,2},{2,0},{4,6},{6,4},{1,3},{3,1},{5,7},{7,5},{8,10},{10,8},{12,... | collective-permute-start | bytes 442376 | tf_op jit(solution)/shard_map/ppermute | solution.py:212
  104.0 2.6 %collective-permute-start.41 = (bf16[72,1024]{1,0:T(8,128)(2,1)S(1)}, bf16[72,1024]{1,0:T(8,128)(2,1)S(1)}, u32[]{:S(2)}, u32[]{:S(2)}) collective-permute-start(bf16[72,1024]{1,0:T(8,128)(2,1)S(1)} %get-tuple-element.94), channel_id=1, source_target_pairs={{0,6},{2,4},{4,2},{6,0},{1,7},{3,5},{5,3},{7,1},{8,14},{10,12},{12... | collective-permute-start | bytes 442376 | tf_op jit(solution)/shard_map/ppermute | solution.py:212
  107.1 1.9 %collective-permute-start.31 = (bf16[72,1024]{1,0:T(8,128)(2,1)S(1)}, bf16[72,1024]{1,0:T(8,128)(2,1)S(1)}, u32[]{:S(2)}, u32[]{:S(2)}) collective-permute-start(bf16[72,1024]{1,0:T(8,128)(2,1)S(1)} %get-tuple-element.84), channel_id=1, source_target_pairs={{0,2},{2,0},{4,6},{6,4},{1,3},{3,1},{5,7},{7,5},{8,10},{10,8},{12,... | collective-permute-start | bytes 442376 | tf_op jit(solution)/shard_map/ppermute | solution.py:212
  109.0 8.4 %collective-permute-done.40.refs_2_ = bf16[72,1024]{1,0:T(8,128)(2,1)S(1)} collective-permute-done((bf16[72,1024]{1,0:T(8,128)(2,1)S(1)}, bf16[72,1024]{1,0:T(8,128)(2,1)S(1)}, u32[]{:S(2)}, u32[]{:S(2)}) %collective-permute-start.40) | collective-permute-done | bytes 147488 | tf_op jit(solution)/shard_map/ppermute | solution.py:212
  119.5 2.0 %collective-permute-start.36 = (bf16[72,1024]{1,0:T(8,128)(2,1)S(1)}, bf16[72,1024]{1,0:T(8,128)(2,1)S(1)}, u32[]{:S(2)}, u32[]{:S(2)}) collective-permute-start(bf16[72,1024]{1,0:T(8,128)(2,1)S(1)} %get-tuple-element.88), channel_id=1, source_target_pairs={{0,2},{2,0},{4,6},{6,4},{1,3},{3,1},{5,7},{7,5},{8,10},{10,8},{12,... | collective-permute-start | bytes 442376 | tf_op jit(solution)/shard_map/ppermute | solution.py:212
  122.1 2.1 %collective-permute-done.32.refs_2_ = bf16[72,1024]{1,0:T(8,128)(2,1)S(1)} collective-permute-done((bf16[72,1024]{1,0:T(8,128)(2,1)S(1)}, bf16[72,1024]{1,0:T(8,128)(2,1)S(1)}, u32[]{:S(2)}, u32[]{:S(2)}) %collective-permute-start.32) | collective-permute-done | bytes 147488 | tf_op jit(solution)/shard_map/ppermute | solution.py:212
  124.1 3.3 %collective-permute-start.42 = (bf16[128,1024]{1,0:T(8,128)(2,1)S(1)}, bf16[128,1024]{1,0:T(8,128)(2,1)S(1)}, u32[]{:S(2)}, u32[]{:S(2)}) collective-permute-start(bf16[128,1024]{1,0:T(8,128)(2,1)S(1)} %shard_map.98), channel_id=1, source_target_pairs={{0,8},{8,0},{16,24},{24,16},{1,9},{9,1},{17,25},{25,17},{2,10},{10... | collective-permute-start | bytes 786440 | tf_op jit(solution)/shard_map/ppermute | solution.py:212
  127.5 3.4 %expert.4 = (bf16[72,2048]{1,0:T(8,128)(2,1)S(1)}, bf16[72,2048]{1,0:T(8,128)(2,1)S(1)}, bf16[72,2048]{1,0:T(8,128)(2,1)S(1)}, bf16[72,2048]{1,0:T(8,128)(2,1)S(1)}) custom-call(s32[3]{0:T(128)S(1)} %pad_add_fusion.1.expert_ref.scal_ref, s32[2]{0:T(128)S(1)} %bitcast.34, bf16[1160,128]{1,0:T(8,128)(2,1)S(1)} %get-tuple-element.51.refs_0_, ...), custom_call_target="tpu_custom_call" | custom-call | flops 1358954496 | bytes 4718592 | tf_op jit(solution)/shard_map/expert/pallas_call | solution.py:336
  130.8 2.0 %collective-permute-start.7 = (bf16[72,2048]{1,0:T(8,128)(2,1)S(1)}, bf16[72,2048]{1,0:T(8,128)(2,1)S(1)}, u32[]{:S(2)}, u32[]{:S(2)}) collective-permute-start(bf16[72,2048]{1,0:T(8,128)(2,1)S(1)} %get-tuple-element.56), channel_id=1, source_target_pairs={{0,2},{2,0},{4,6},{6,4},{1,3},{3,1},{5,7},{7,5},{8,10},{10,8},{12,... | collective-permute-start | bytes 884744 | tf_op jit(solution)/shard_map/ppermute | solution.py:212
  134.2 2.1 %collective-permute-start.17 = (bf16[128,2048]{1,0:T(8,128)(2,1)S(1)}, bf16[128,2048]{1,0:T(8,128)(2,1)S(1)}, u32[]{:S(2)}, u32[]{:S(2)}) collective-permute-start(bf16[128,2048]{1,0:T(8,128)(2,1)S(1)} %shard_map.93), channel_id=1, source_target_pairs={{0,8},{8,0},{16,24},{24,16},{1,9},{9,1},{17,25},{25,17},{2,10},{10... | collective-permute-start | bytes 1572872 | tf_op jit(solution)/shard_map/ppermute | solution.py:212
  136.9 6.0 %collective-permute-done.38.refs_3_ = bf16[72,1024]{1,0:T(8,128)(2,1)S(1)} collective-permute-done((bf16[72,1024]{1,0:T(8,128)(2,1)S(1)}, bf16[72,1024]{1,0:T(8,128)(2,1)S(1)}, u32[]{:S(2)}, u32[]{:S(2)}) %collective-permute-start.38) | collective-permute-done | bytes 147488 | tf_op jit(solution)/shard_map/ppermute | solution.py:212
  143.8 2.5 %collective-permute-start.9 = (bf16[72,2048]{1,0:T(8,128)(2,1)S(1)}, bf16[72,2048]{1,0:T(8,128)(2,1)S(1)}, u32[]{:S(2)}, u32[]{:S(2)}) collective-permute-start(bf16[72,2048]{1,0:T(8,128)(2,1)S(1)} %get-tuple-element.58), channel_id=1, source_target_pairs={{0,6},{2,4},{4,2},{6,0},{1,7},{3,5},{5,3},{7,1},{8,14},{10,12},{12... | collective-permute-start | bytes 884744 | tf_op jit(solution)/shard_map/ppermute | solution.py:212
  147.5 3.0 %collective-permute-start.35 = (bf16[128,1024]{1,0:T(8,128)(2,1)S(1)}, bf16[128,1024]{1,0:T(8,128)(2,1)S(1)}, u32[]{:S(2)}, u32[]{:S(2)}) collective-permute-start(bf16[128,1024]{1,0:T(8,128)(2,1)S(1)} %shard_map.97), channel_id=1, source_target_pairs={{0,16},{8,24},{16,0},{24,8},{1,17},{9,25},{17,1},{25,9},{2,18},{10... | collective-permute-start | bytes 786440 | tf_op jit(solution)/shard_map/ppermute | solution.py:212
  150.4 2.3 %collective-permute-done.8.refs_2_ = bf16[72,2048]{1,0:T(8,128)(2,1)S(1)} collective-permute-done((bf16[72,2048]{1,0:T(8,128)(2,1)S(1)}, bf16[72,2048]{1,0:T(8,128)(2,1)S(1)}, u32[]{:S(2)}, u32[]{:S(2)}) %collective-permute-start.8) | collective-permute-done | bytes 294944 | tf_op jit(solution)/shard_map/ppermute | solution.py:212
  153.5 6.3 %collective-permute-done.43.refs_2_ = bf16[128,1024]{1,0:T(8,128)(2,1)S(1)} collective-permute-done((bf16[128,1024]{1,0:T(8,128)(2,1)S(1)}, bf16[128,1024]{1,0:T(8,128)(2,1)S(1)}, u32[]{:S(2)}, u32[]{:S(2)}) %collective-permute-start.43) | collective-permute-done | bytes 262176 | tf_op jit(solution)/shard_map/ppermute | solution.py:212
  159.8 2.8 %collective-permute-done.35.refs_1_ = bf16[128,1024]{1,0:T(8,128)(2,1)S(1)} collective-permute-done((bf16[128,1024]{1,0:T(8,128)(2,1)S(1)}, bf16[128,1024]{1,0:T(8,128)(2,1)S(1)}, u32[]{:S(2)}, u32[]{:S(2)}) %collective-permute-start.35) | collective-permute-done | bytes 262176 | tf_op jit(solution)/shard_map/ppermute | solution.py:212
  (85 shorter events, 39.8 us)
Async XLA Ops:
  3.5 15.7 %collective-permute-start.10 = (bf16[128,2176]{1,0:T(8,128)(2,1)S(1)}, bf16[128,2176]{1,0:T(8,128)(2,1)S(1)}, u32[]{:S(2)}, u32[]{:S(2)}) collective-permute-start(bf16[128,2176]{1,0:T(8,128)(2,1)S(1)} %get-tuple-element.59), channel_id=1, source_target_pairs={{0,8},{8,0},{16,24},{24,16},{1,9},{9,1},{17,25},{25,17},{2,10},{10... | collective-permute-start | bytes 1671176 | tf_op jit(solution)/shard_map/ppermute | solution.py:212
  6.7 16.6 %collective-permute-start.19 = (bf16[128,2176]{1,0:T(8,128)(2,1)S(1)}, bf16[128,2176]{1,0:T(8,128)(2,1)S(1)}, u32[]{:S(2)}, u32[]{:S(2)}) collective-permute-start(bf16[128,2176]{1,0:T(8,128)(2,1)S(1)} %get-tuple-element.59), channel_id=1, source_target_pairs={{8,16},{16,8},{9,17},{17,9},{10,18},{18,10},{11,19},{19,11},{12,20... | collective-permute-start | bytes 1671176 | tf_op jit(solution)/shard_map/ppermute | solution.py:217
  7.3 69.8 %collective-permute-start.3 = (bf16[1024,768]{1,0:T(8,128)(2,1)}, bf16[1024,768]{1,0:T(8,128)(2,1)S(1)}, u32[]{:S(2)}, u32[]{:S(2)}) collective-permute-start(bf16[1024,768]{1,0:T(8,128)(2,1)} %bitcast.11), channel_id=1, source_target_pairs={{0,1},{1,0},{2,3},{3,2},{4,5},{5,4},{6,7},{7,6},{8,9},{9,8},{10,11... | collective-permute-start | bytes 4718600 | tf_op jit(solution)/shard_map/ppermute | solution.py:212
  19.3 13.3 %collective-permute-start.18 = (bf16[128,2176]{1,0:T(8,128)(2,1)S(1)}, bf16[128,2176]{1,0:T(8,128)(2,1)S(1)}, u32[]{:S(2)}, u32[]{:S(2)}) collective-permute-start(bf16[128,2176]{1,0:T(8,128)(2,1)S(1)} %collective-permute-done.10.refs_0_), channel_id=1, source_target_pairs={{8,16},{16,8},{9,17},{17,9},{10,18},{18,10},{11,19},{19,11},{12,20... | collective-permute-start | bytes 1671176 | tf_op jit(solution)/shard_map/ppermute | solution.py:217
  23.3 19.1 %collective-permute-start.20 = (bf16[128,2176]{1,0:T(8,128)(2,1)S(1)}, bf16[128,2176]{1,0:T(8,128)(2,1)S(1)}, u32[]{:S(2)}, u32[]{:S(2)}) collective-permute-start(bf16[128,2176]{1,0:T(8,128)(2,1)S(1)} %collective-permute-done.19.refs_0_), channel_id=1, source_target_pairs={{8,0},{16,24},{9,1},{17,25},{10,2},{18,26},{11,3},{19,27},{12,4},{... | collective-permute-start | bytes 1671176 | tf_op jit(solution)/shard_map/ppermute | solution.py:217
  24.6 20.8 %collective-permute-start.4 = (bf16[384,1024]{1,0:T(8,128)(2,1)}, bf16[384,1024]{1,0:T(8,128)(2,1)S(1)}, u32[]{:S(2)}, u32[]{:S(2)}) collective-permute-start(bf16[384,1024]{1,0:T(8,128)(2,1)} %bitcast.16), channel_id=1, source_target_pairs={{0,1},{1,0},{2,3},{3,2},{4,5},{5,4},{6,7},{7,6},{8,9},{9,8},{10,11... | collective-permute-start | bytes 2359304 | tf_op jit(solution)/shard_map/ppermute | solution.py:212
  32.6 25.8 %collective-permute-start.27 = (bf16[128,2176]{1,0:T(8,128)(2,1)S(1)}, bf16[128,2176]{1,0:T(8,128)(2,1)S(1)}, u32[]{:S(2)}, u32[]{:S(2)}) collective-permute-start(bf16[128,2176]{1,0:T(8,128)(2,1)S(1)} %collective-permute-done.18.refs_0_), channel_id=1, source_target_pairs={{8,0},{16,24},{9,1},{17,25},{10,2},{18,26},{11,3},{19,27},{12,4},{... | collective-permute-start | bytes 1671176 | tf_op jit(solution)/shard_map/ppermute | solution.py:217
  42.4 14.5 %collective-permute-start.12 = (bf16[1160,128]{1,0:T(8,128)(2,1)S(1)}, bf16[1160,128]{1,0:T(8,128)(2,1)S(1)}, u32[]{:S(2)}, u32[]{:S(2)}) collective-permute-start(bf16[1160,128]{1,0:T(8,128)(2,1)S(1)} %get-tuple-element.63), channel_id=1, source_target_pairs={{0,4},{2,6},{4,0},{6,2},{1,5},{3,7},{5,1},{7,3},{8,12},{10,14},{12... | collective-permute-start | bytes 890888 | tf_op jit(solution)/shard_map/ppermute | solution.py:212
  45.4 16.2 %collective-permute-start.13 = (bf16[1160,128]{1,0:T(8,128)(2,1)S(1)}, bf16[1160,128]{1,0:T(8,128)(2,1)S(1)}, u32[]{:S(2)}, u32[]{:S(2)}) collective-permute-start(bf16[1160,128]{1,0:T(8,128)(2,1)S(1)} %get-tuple-element.64), channel_id=1, source_target_pairs={{0,6},{2,4},{4,2},{6,0},{1,7},{3,5},{5,3},{7,1},{8,14},{10,12},{12... | collective-permute-start | bytes 890888 | tf_op jit(solution)/shard_map/ppermute | solution.py:212
  47.5 14.7 %collective-permute-start.21 = (bf16[1160,128]{1,0:T(8,128)(2,1)S(1)}, bf16[1160,128]{1,0:T(8,128)(2,1)S(1)}, u32[]{:S(2)}, u32[]{:S(2)}) collective-permute-start(bf16[1160,128]{1,0:T(8,128)(2,1)S(1)} %get-tuple-element.71), channel_id=1, source_target_pairs={{0,2},{2,0},{4,6},{6,4},{1,3},{3,1},{5,7},{7,5},{8,10},{10,8},{12,... | collective-permute-start | bytes 890888 | tf_op jit(solution)/shard_map/ppermute | solution.py:212
  56.9 16.4 %collective-permute-start.22 = (bf16[1160,128]{1,0:T(8,128)(2,1)S(1)}, bf16[1160,128]{1,0:T(8,128)(2,1)S(1)}, u32[]{:S(2)}, u32[]{:S(2)}) collective-permute-start(bf16[1160,128]{1,0:T(8,128)(2,1)S(1)} %get-tuple-element.72), channel_id=1, source_target_pairs={{0,4},{2,6},{4,0},{6,2},{1,5},{3,7},{5,1},{7,3},{8,12},{10,14},{12... | collective-permute-start | bytes 890888 | tf_op jit(solution)/shard_map/ppermute | solution.py:212
  58.4 22.0 %collective-permute-start.23 = (bf16[1160,128]{1,0:T(8,128)(2,1)S(1)}, bf16[1160,128]{1,0:T(8,128)(2,1)S(1)}, u32[]{:S(2)}, u32[]{:S(2)}) collective-permute-start(bf16[1160,128]{1,0:T(8,128)(2,1)S(1)} %get-tuple-element.73), channel_id=1, source_target_pairs={{0,6},{2,4},{4,2},{6,0},{1,7},{3,5},{5,3},{7,1},{8,14},{10,12},{12... | collective-permute-start | bytes 890888 | tf_op jit(solution)/shard_map/ppermute | solution.py:212
  61.6 23.7 %collective-permute-start.28 = (bf16[1160,128]{1,0:T(8,128)(2,1)S(1)}, bf16[1160,128]{1,0:T(8,128)(2,1)S(1)}, u32[]{:S(2)}, u32[]{:S(2)}) collective-permute-start(bf16[1160,128]{1,0:T(8,128)(2,1)S(1)} %get-tuple-element.80), channel_id=1, source_target_pairs={{0,2},{2,0},{4,6},{6,4},{1,3},{3,1},{5,7},{7,5},{8,10},{10,8},{12,... | collective-permute-start | bytes 890888 | tf_op jit(solution)/shard_map/ppermute | solution.py:212
  62.3 24.9 %collective-permute-start.29 = (bf16[1160,128]{1,0:T(8,128)(2,1)S(1)}, bf16[1160,128]{1,0:T(8,128)(2,1)S(1)}, u32[]{:S(2)}, u32[]{:S(2)}) collective-permute-start(bf16[1160,128]{1,0:T(8,128)(2,1)S(1)} %get-tuple-element.81), channel_id=1, source_target_pairs={{0,4},{2,6},{4,0},{6,2},{1,5},{3,7},{5,1},{7,3},{8,12},{10,14},{12... | collective-permute-start | bytes 890888 | tf_op jit(solution)/shard_map/ppermute | solution.py:212
  73.4 16.3 %collective-permute-start.30 = (bf16[1160,128]{1,0:T(8,128)(2,1)S(1)}, bf16[1160,128]{1,0:T(8,128)(2,1)S(1)}, u32[]{:S(2)}, u32[]{:S(2)}) collective-permute-start(bf16[1160,128]{1,0:T(8,128)(2,1)S(1)} %get-tuple-element.82), channel_id=1, source_target_pairs={{0,6},{2,4},{4,2},{6,0},{1,7},{3,5},{5,3},{7,1},{8,14},{10,12},{12... | collective-permute-start | bytes 890888 | tf_op jit(solution)/shard_map/ppermute | solution.py:212
  77.1 18.6 %collective-permute-start.2 = (bf16[1160,128]{1,0:T(8,128)(2,1)S(1)}, bf16[1160,128]{1,0:T(8,128)(2,1)S(1)}, u32[]{:S(2)}, u32[]{:S(2)}) collective-permute-start(bf16[1160,128]{1,0:T(8,128)(2,1)S(1)} %get-tuple-element.54), channel_id=1, source_target_pairs={{0,6},{2,4},{4,2},{6,0},{1,7},{3,5},{5,3},{7,1},{8,14},{10,12},{12... | collective-permute-start | bytes 890888 | tf_op jit(solution)/shard_map/ppermute | solution.py:212
  80.4 26.2 %collective-permute-start.14 = (bf16[72,2048]{1,0:T(8,128)(2,1)S(1)}, bf16[72,2048]{1,0:T(8,128)(2,1)S(1)}, u32[]{:S(2)}, u32[]{:S(2)}) collective-permute-start(bf16[72,2048]{1,0:T(8,128)(2,1)S(1)} %get-tuple-element.66), channel_id=1, source_target_pairs={{0,2},{2,0},{4,6},{6,4},{1,3},{3,1},{5,7},{7,5},{8,10},{10,8},{12,... | collective-permute-start | bytes 884744 | tf_op jit(solution)/shard_map/ppermute | solution.py:212
  85.4 14.6 %collective-permute-start.24 = (bf16[72,1024]{1,0:T(8,128)(2,1)S(1)}, bf16[72,1024]{1,0:T(8,128)(2,1)S(1)}, u32[]{:S(2)}, u32[]{:S(2)}) collective-permute-start(bf16[72,1024]{1,0:T(8,128)(2,1)S(1)} %get-tuple-element.75), channel_id=1, source_target_pairs={{0,2},{2,0},{4,6},{6,4},{1,3},{3,1},{5,7},{7,5},{8,10},{10,8},{12,... | collective-permute-start | bytes 442376 | tf_op jit(solution)/shard_map/ppermute | solution.py:212
  87.2 15.2 %collective-permute-start.25 = (bf16[72,1024]{1,0:T(8,128)(2,1)S(1)}, bf16[72,1024]{1,0:T(8,128)(2,1)S(1)}, u32[]{:S(2)}, u32[]{:S(2)}) collective-permute-start(bf16[72,1024]{1,0:T(8,128)(2,1)S(1)} %get-tuple-element.76), channel_id=1, source_target_pairs={{0,4},{2,6},{4,0},{6,2},{1,5},{3,7},{5,1},{7,3},{8,12},{10,14},{12... | collective-permute-start | bytes 442376 | tf_op jit(solution)/shard_map/ppermute | solution.py:212
  89.6 14.3 %collective-permute-start.26 = (bf16[72,1024]{1,0:T(8,128)(2,1)S(1)}, bf16[72,1024]{1,0:T(8,128)(2,1)S(1)}, u32[]{:S(2)}, u32[]{:S(2)}) collective-permute-start(bf16[72,1024]{1,0:T(8,128)(2,1)S(1)} %get-tuple-element.77), channel_id=1, source_target_pairs={{0,6},{2,4},{4,2},{6,0},{1,7},{3,5},{5,3},{7,1},{8,14},{10,12},{12... | collective-permute-start | bytes 442376 | tf_op jit(solution)/shard_map/ppermute | solution.py:212
  95.8 23.7 %collective-permute-start.15 = (bf16[72,2048]{1,0:T(8,128)(2,1)S(1)}, bf16[72,2048]{1,0:T(8,128)(2,1)S(1)}, u32[]{:S(2)}, u32[]{:S(2)}) collective-permute-start(bf16[72,2048]{1,0:T(8,128)(2,1)S(1)} %get-tuple-element.67), channel_id=1, source_target_pairs={{0,4},{2,6},{4,0},{6,2},{1,5},{3,7},{5,1},{7,3},{8,12},{10,14},{12... | collective-permute-start | bytes 884744 | tf_op jit(solution)/shard_map/ppermute | solution.py:212
  102.4 15.0 %collective-permute-start.40 = (bf16[72,1024]{1,0:T(8,128)(2,1)S(1)}, bf16[72,1024]{1,0:T(8,128)(2,1)S(1)}, u32[]{:S(2)}, u32[]{:S(2)}) collective-permute-start(bf16[72,1024]{1,0:T(8,128)(2,1)S(1)} %get-tuple-element.93), channel_id=1, source_target_pairs={{0,4},{2,6},{4,0},{6,2},{1,5},{3,7},{5,1},{7,3},{8,12},{10,14},{12... | collective-permute-start | bytes 442376 | tf_op jit(solution)/shard_map/ppermute | solution.py:212
  104.0 14.0 %collective-permute-start.41 = (bf16[72,1024]{1,0:T(8,128)(2,1)S(1)}, bf16[72,1024]{1,0:T(8,128)(2,1)S(1)}, u32[]{:S(2)}, u32[]{:S(2)}) collective-permute-start(bf16[72,1024]{1,0:T(8,128)(2,1)S(1)} %get-tuple-element.94), channel_id=1, source_target_pairs={{0,6},{2,4},{4,2},{6,0},{1,7},{3,5},{5,3},{7,1},{8,14},{10,12},{12... | collective-permute-start | bytes 442376 | tf_op jit(solution)/shard_map/ppermute | solution.py:212
  106.6 26.8 %collective-permute-start.16 = (bf16[72,2048]{1,0:T(8,128)(2,1)S(1)}, bf16[72,2048]{1,0:T(8,128)(2,1)S(1)}, u32[]{:S(2)}, u32[]{:S(2)}) collective-permute-start(bf16[72,2048]{1,0:T(8,128)(2,1)S(1)} %get-tuple-element.68), channel_id=1, source_target_pairs={{0,6},{2,4},{4,2},{6,0},{1,7},{3,5},{5,3},{7,1},{8,14},{10,12},{12... | collective-permute-start | bytes 884744 | tf_op jit(solution)/shard_map/ppermute | solution.py:212
  107.1 14.4 %collective-permute-start.31 = (bf16[72,1024]{1,0:T(8,128)(2,1)S(1)}, bf16[72,1024]{1,0:T(8,128)(2,1)S(1)}, u32[]{:S(2)}, u32[]{:S(2)}) collective-permute-start(bf16[72,1024]{1,0:T(8,128)(2,1)S(1)} %get-tuple-element.84), channel_id=1, source_target_pairs={{0,2},{2,0},{4,6},{6,4},{1,3},{3,1},{5,7},{7,5},{8,10},{10,8},{12,... | collective-permute-start | bytes 442376 | tf_op jit(solution)/shard_map/ppermute | solution.py:212
  119.5 14.7 %collective-permute-start.36 = (bf16[72,1024]{1,0:T(8,128)(2,1)S(1)}, bf16[72,1024]{1,0:T(8,128)(2,1)S(1)}, u32[]{:S(2)}, u32[]{:S(2)}) collective-permute-start(bf16[72,1024]{1,0:T(8,128)(2,1)S(1)} %get-tuple-element.88), channel_id=1, source_target_pairs={{0,2},{2,0},{4,6},{6,4},{1,3},{3,1},{5,7},{7,5},{8,10},{10,8},{12,... | collective-permute-start | bytes 442376 | tf_op jit(solution)/shard_map/ppermute | solution.py:212
  121.5 14.8 %collective-permute-start.37 = (bf16[72,1024]{1,0:T(8,128)(2,1)S(1)}, bf16[72,1024]{1,0:T(8,128)(2,1)S(1)}, u32[]{:S(2)}, u32[]{:S(2)}) collective-permute-start(bf16[72,1024]{1,0:T(8,128)(2,1)S(1)} %get-tuple-element.89), channel_id=1, source_target_pairs={{0,4},{2,6},{4,0},{6,2},{1,5},{3,7},{5,1},{7,3},{8,12},{10,14},{12... | collective-permute-start | bytes 442376 | tf_op jit(solution)/shard_map/ppermute | solution.py:212
  124.1 19.7 %collective-permute-start.42 = (bf16[128,1024]{1,0:T(8,128)(2,1)S(1)}, bf16[128,1024]{1,0:T(8,128)(2,1)S(1)}, u32[]{:S(2)}, u32[]{:S(2)}) collective-permute-start(bf16[128,1024]{1,0:T(8,128)(2,1)S(1)} %shard_map.98), channel_id=1, source_target_pairs={{0,8},{8,0},{16,24},{24,16},{1,9},{9,1},{17,25},{25,17},{2,10},{10... | collective-permute-start | bytes 786440 | tf_op jit(solution)/shard_map/ppermute | solution.py:212
  130.8 16.6 %collective-permute-start.7 = (bf16[72,2048]{1,0:T(8,128)(2,1)S(1)}, bf16[72,2048]{1,0:T(8,128)(2,1)S(1)}, u32[]{:S(2)}, u32[]{:S(2)}) collective-permute-start(bf16[72,2048]{1,0:T(8,128)(2,1)S(1)} %get-tuple-element.56), channel_id=1, source_target_pairs={{0,2},{2,0},{4,6},{6,4},{1,3},{3,1},{5,7},{7,5},{8,10},{10,8},{12,... | collective-permute-start | bytes 884744 | tf_op jit(solution)/shard_map/ppermute | solution.py:212
  133.4 13.5 %collective-permute-start.34 = (bf16[128,1024]{1,0:T(8,128)(2,1)S(1)}, bf16[128,1024]{1,0:T(8,128)(2,1)S(1)}, u32[]{:S(2)}, u32[]{:S(2)}) collective-permute-start(bf16[128,1024]{1,0:T(8,128)(2,1)S(1)} %shard_map.96), channel_id=1, source_target_pairs={{0,8},{8,0},{16,24},{24,16},{1,9},{9,1},{17,25},{25,17},{2,10},{10... | collective-permute-start | bytes 786440 | tf_op jit(solution)/shard_map/ppermute | solution.py:212
  134.2 19.3 %collective-permute-start.17 = (bf16[128,2048]{1,0:T(8,128)(2,1)S(1)}, bf16[128,2048]{1,0:T(8,128)(2,1)S(1)}, u32[]{:S(2)}, u32[]{:S(2)}) collective-permute-start(bf16[128,2048]{1,0:T(8,128)(2,1)S(1)} %shard_map.93), channel_id=1, source_target_pairs={{0,8},{8,0},{16,24},{24,16},{1,9},{9,1},{17,25},{25,17},{2,10},{10... | collective-permute-start | bytes 1572872 | tf_op jit(solution)/shard_map/ppermute | solution.py:212
  147.5 15.2 %collective-permute-start.35 = (bf16[128,1024]{1,0:T(8,128)(2,1)S(1)}, bf16[128,1024]{1,0:T(8,128)(2,1)S(1)}, u32[]{:S(2)}, u32[]{:S(2)}) collective-permute-start(bf16[128,1024]{1,0:T(8,128)(2,1)S(1)} %shard_map.97), channel_id=1, source_target_pairs={{0,16},{8,24},{16,0},{24,8},{1,17},{9,25},{17,1},{25,9},{2,18},{10... | collective-permute-start | bytes 786440 | tf_op jit(solution)/shard_map/ppermute | solution.py:212
  (18 other events, 474.8 us)
